TPU v7x, 32 devices: a whole 2x2x4 slice. The times are simulated.
32 devices in a mesh: grp: 4 (over y, x), sub: 8 (over z, core).
Axes of the slice: x: 2, y: 2, z: 4, core: 2. Of those that a mesh axis runs over, the one named last changes fastest.
Arguments:
- initial_field: float32 [4, 16, 16384], P('grp', 'sub'), may hold values from -6 to 6
- conduct: float32 [4, 16, 16384], P('grp', 'sub'), may hold values from 0.02 to 0.12
- velocity: float32 [4, 16, 16384], P('grp', 'sub'), may hold values from 0 to 0.25
- heat_release: float32 [4, 16, 16384], P('grp', 'sub'), may hold values from 0.01 to 0.1
- group_kind: int32 [4], replicated, may hold values from 0 to 1, as said below
- partner: int32 [4], replicated, may hold values from 0 to 3, as said below
- surface_cell: int32 [4, 4096], P('grp', 'sub'), may hold values from 0 to 32767
- patch_count: int32 [4, 8], P('grp'), may hold values from 1 to 24, 64 in all within a row
- patch_centres: int32 [4, 192, 128], P('grp', 'sub'), may hold values from 0 to 4095, as said below
- patch_targets: int32 [4, 192, 128], P('grp', 'sub'), may hold values from 0 to 4095
- patch_maps: float32 [4, 192, 128, 128], P('grp', 'sub'), may hold values from -0.25 to 0.95
Outputs:
- temperature: float32 [4, 16, 16384], P('grp', 'sub')
- interface: float32 [4, 2, 4096], P('grp', None, 'sub')
Inputs may be any that keep to these rules, and one draw needn't show every extreme that they name: `group_kind`: both kinds occur. partner[g] is a group of the other kind than g. Slots 0 to patch_count[g, j] - 1 of device j of group g are live; each group's counts sum to 64; in each group some device holds 24. `patch_centres`: the centres of slot s of group g lie in the cyclic window of 1024 consecutive nodes that starts at (s // 24) * 512 - 512 // 2 + h[g], for one shift h[g] of each group.
All inputs are finite; a program needn't handle non-finite values.
Results may differ from a plain program's by a relative error of at most 0.00013.
Values sent between devices are 32-bit elements; how exact they have to be, the bound alone decides.
A program may use at most 64 MiB of HBM per device.

v0:
```python
import jax
import jax.numpy as jnp
from jax import lax
from jax.experimental import pallas as pl
from jax.experimental.pallas import tpu as pltpu
from jax.sharding import PartitionSpec as P

STEPS = 4
COUPLE = 4
LANES = 128
F32 = jnp.float32
BF16 = jnp.bfloat16


def split(x):
    hi = x.astype(BF16).astype(F32)
    return hi, x - hi


def dot_nt(a, b):
    return lax.dot_general(a, b, (((1,), (1,)), ((), ())), preferred_element_type=F32)


def dot_nn(a, b):
    return lax.dot_general(a, b, (((1,), (0,)), ((), ())), preferred_element_type=F32)


def iota(shape, dim):
    return lax.broadcasted_iota(jnp.int32, shape, dim)


def in_plane(c):
    rows, cols = c.shape
    return (
        pltpu.roll(c, 1, 0)
        + pltpu.roll(c, rows - 1, 0)
        + pltpu.roll(c, 1, 1)
        + pltpu.roll(c, cols - 1, 1)
    )


def kernel(
    n,
    groups,
    kind_ref,
    partner_ref,
    count_ref,
    field_ref,
    cond_ref,
    vel_ref,
    heat_ref,
    surf_ref,
    cent_ref,
    targ_ref,
    maps_ref,
    out_ref,
    iface_ref,
    fa,
    fb,
    cx,
    vx,
    hx,
    land,
    surf_all,
    oh_surf,
    oh_cent,
    oh_targ,
    maps2,
    exp_buf,
    grp_land,
    sel_buf,
    gath,
    part,
    rs_land,
    inc_buf,
    inc_land,
    set_send,
    set_recv,
    grp_send,
    grp_recv,
    ga_send,
    ga_recv,
    rs_send,
    rs_recv,
    inc_send,
    inc_recv,
    halo_send,
    halo_recv,
    maps,
    load_sem,
):
    planes = field_ref.shape[1]
    rows = fa.shape[1]
    near = STEPS // 2
    assert near % 2 == 0 and near <= planes
    surf_here = surf_ref.shape[1]
    cap = cent_ref.shape[0]
    reach = -(-STEPS // planes)
    depth = reach * planes
    ext = planes + 2 * depth
    offs = [d for d in range(-reach, reach + 1) if d != 0]
    at = {d: i for i, d in enumerate(offs)}
    tile = 2 * surf_here // LANES
    half = surf_here // LANES
    me = lax.axis_index("sub")
    grp = lax.axis_index("grp")

    def there(d):
        return jnp.logical_and(me + d >= 0, me + d < n)

    def rcopy(src, dst, ss, rs, dev):
        return pltpu.make_async_remote_copy(
            src_ref=src,
            dst_ref=dst,
            send_sem=ss,
            recv_sem=rs,
            device_id=dev,
            device_id_type=pl.DeviceIdType.MESH,
        )

    load = pltpu.make_async_copy(maps_ref, maps, load_sem)
    load.start()

    for buf in (fa, cx, vx, hx):
        buf[...] = jnp.zeros(buf.shape, F32)
    land[...] = jnp.zeros(land.shape, F32)
    inc_land[...] = jnp.zeros(inc_land.shape, F32)
    surf_all[...] = jnp.zeros(surf_all.shape, jnp.int32)

    barrier = pltpu.get_barrier_semaphore()
    for k in range(1, n):
        pl.semaphore_signal(
            barrier, inc=1, device_id={"sub": lax.rem(me + k, n)}, device_id_type=pl.DeviceIdType.MESH
        )
    for k in range(1, groups):
        pl.semaphore_signal(
            barrier, inc=1, device_id={"grp": lax.rem(grp + k, groups)}, device_id_type=pl.DeviceIdType.MESH
        )

    own = pl.ds(depth, planes)
    fetch = ((field_ref, fa), (cond_ref, cx), (vel_ref, vx), (heat_ref, hx))

    def unfold(b, carry):
        chunk = pl.ds(pl.multiple_of(b * 8 * LANES, LANES), 8 * LANES)
        for src, dst in fetch:
            x = src[0, :, chunk]
            for p in range(planes):
                dst[depth + p, pl.ds(pl.multiple_of(b * 8, 8), 8), :] = jnp.concatenate(
                    [x[p : p + 1, i * LANES : (i + 1) * LANES] for i in range(8)], axis=0
                )
        return carry

    lax.fori_loop(0, rows // 8, unfold, 0)
    pl.semaphore_wait(barrier, n - 1 + groups - 1)

    def send_planes(buf, lo, hi, to, j):
        slot = -to
        shift = depth - (depth + planes * slot)
        return rcopy(
            buf.at[pl.ds(lo + shift, hi - lo)],
            buf.at[pl.ds(lo, hi - lo)],
            set_send.at[j, at[to]],
            set_recv.at[j, at[slot]],
            {"sub": me + to},
        )

    def first_copies(to):
        base = depth - planes * to
        lo, hi = max(base, depth - near), min(base + planes, depth + planes + near)
        out = [send_planes(fa, lo, hi, to, 0)]
        lo, hi = max(base, depth - near + 1), min(base + planes, depth + planes + near - 1)
        if hi > lo:
            out += [send_planes(buf, lo, hi, to, j + 1) for j, buf in enumerate((cx, vx, hx))]
        return out

    def rest_copies(to, which):
        base = depth - planes * to
        lo, hi = max(base, 1), min(base + planes, ext - 1)
        if to == 1:
            hi = min(hi, depth - near + 1)
        if to == -1:
            lo = max(lo, depth + planes + near - 1)
        if hi <= lo:
            return []
        return [send_planes((cx, vx, hx)[j], lo, hi, to, j + 4) for j in which]

    def surf_copies(to):
        return [
            rcopy(
                surf_ref,
                surf_all.at[reach - to],
                set_send.at[7, at[to]],
                set_recv.at[7, at[-to]],
                {"sub": me + to},
            )
        ]

    def mid_copy(to):
        return rcopy(
            fa.at[own],
            land.at[1, at[-to]],
            set_send.at[8, at[to]],
            set_recv.at[8, at[-to]],
            {"sub": me + to},
        )

    def each(ds, act):
        for d in ds:

            @pl.when(there(d))
            def _():
                act(d)

    def starts(copies):
        for c in copies:
            c.start()

    def arrivals(copies):
        for c in copies:
            c.wait_recv()

    def departures(copies):
        for c in copies:
            c.wait_send()

    beside = (-1, 1)
    each(beside, lambda d: starts(first_copies(d)))

    kind = kind_ref[grp]
    gas = jnp.where(kind == 0, 1.0, 0.0).astype(F32)
    gain_t = jnp.where(kind == 0, 0.5, 0.25).astype(F32)
    gain_f = jnp.where(kind == 0, -0.25, 0.25).astype(F32)
    partner = partner_ref[grp]
    count = count_ref[0, me]
    surf_all[reach] = surf_ref[...]
    node_row = iota((n * tile, LANES), 0)
    node_row = (node_row // tile) * half + node_row % half
    load.wait()
    for s in range(cap):
        lanes = pl.ds(s * LANES, LANES)
        hit = (node_row == cent_ref[s : s + 1, :] // LANES).astype(F32).astype(BF16)
        oh_cent[pl.ds(0, n * tile), lanes] = hit
        oh_cent[pl.ds(n * tile, n * tile), lanes] = hit
        oh_targ[:, lanes] = (node_row == targ_ref[s : s + 1, :] // LANES).astype(F32).astype(BF16)
        live = jnp.where(s < count, 1.0, 0.0).astype(F32)
        hi, lo = split(maps[s] * live)
        maps2[s, pl.ds(0, LANES)] = hi.astype(BF16)
        maps2[s, pl.ds(LANES, LANES)] = lo.astype(BF16)

    cell_row = iota((planes * rows, surf_here), 0)

    def hot_rows(j):
        oh_surf[j] = (cell_row == surf_all[j] // LANES).astype(F32).astype(BF16)

    hot_rows(reach)

    lane_of = iota((LANES, surf_here), 0)
    group_of_slots = 4 if cap % 4 == 0 else 1
    width = group_of_slots * LANES
    lane_of_chunk = iota((LANES, width), 0)
    q_of_row = iota((n * tile, LANES), 0) % tile >= half

    def step(src, dst, k):
        for z in range(k + 1, ext - k - 1):
            c = src[z]
            dn = src[z - 1]
            lap = src[z + 1] + dn + in_plane(c) - 6.0 * c
            dst[z] = c + cx[z] * lap - gas * vx[z] * (c - dn) + gas * hx[z] * jax.nn.sigmoid(2.0 * c)

    def as_row(t8):
        return jnp.concatenate([t8[i : i + 1, :] for i in range(half)], axis=1)

    def spread(slot, t8):
        hi, lo = split(as_row(t8))
        mine = lane_of == surf_all[slot] % LANES
        rhs = jnp.concatenate(
            [jnp.where(mine, hi, 0.0).astype(BF16), jnp.where(mine, lo, 0.0).astype(BF16)], axis=0
        )
        r = dot_nt(oh_surf[slot], rhs)
        return (r[:, :LANES] + r[:, LANES:]).reshape(planes, rows, LANES)

    def halo_copy(par, to, slot):
        return rcopy(
            fa.at[own],
            land.at[par, at[slot]],
            halo_send.at[par, at[to]],
            halo_recv.at[par, at[slot]],
            {"sub": me + to},
        )

    def inc_copy(to, slot):
        return rcopy(
            inc_buf, inc_land.at[at[slot]], inc_send.at[at[to]], inc_recv.at[at[slot]], {"sub": me + to}
        )

    def grp_copy(par, k):
        return rcopy(
            exp_buf,
            grp_land.at[par, k - 1],
            grp_send.at[par, k - 1],
            grp_recv.at[par, k - 1],
            {"grp": lax.rem(grp + k, groups)},
        )

    def gath_copy(k, sender):
        return rcopy(sel_buf, gath.at[sender], ga_send.at[k - 1], ga_recv.at[k - 1], {"sub": lax.rem(me + k, n)})

    def rs_copy(k, sender):
        peer = lax.rem(me + k, n)
        return rcopy(part.at[peer], rs_land.at[sender], rs_send.at[k - 1], rs_recv.at[k - 1], {"sub": peer})

    def couple(it, carry):
        par = lax.rem(it, 2)
        last = it == COUPLE - 1
        first = it == 0
        final = fa

        @pl.when(jnp.logical_not(first))
        def _():
            for k in range(STEPS):
                step(pair[k % 2], pair[(k + 1) % 2], k)

        temp = jnp.concatenate([final[depth + p].T for p in range(planes)], axis=1)
        flux = jnp.concatenate(
            [
                (cx[depth + p] * (4.0 * final[depth + p] - in_plane(final[depth + p]))).T
                for p in range(planes)
            ],
            axis=1,
        )
        pieces = [x.astype(BF16) for v in (temp, flux) for x in split(v)]
        got = dot_nn(jnp.concatenate(pieces, axis=0), oh_surf[reach])
        mine = lane_of == surf_all[reach] % LANES
        for q in range(2):
            v = got[2 * q * LANES : (2 * q + 1) * LANES] + got[(2 * q + 1) * LANES : (2 * q + 2) * LANES]
            v = jnp.sum(jnp.where(mine, v, 0.0), axis=0, keepdims=True)
            for i in range(half):
                exp_buf[q * half + i : q * half + i + 1, :] = v[:, i * LANES : (i + 1) * LANES]

        for k in range(1, groups):
            grp_copy(par, k).start()
        for k in range(1, groups):
            grp_copy(par, k).wait_recv()
        sel = jnp.zeros((tile, LANES), F32)
        for k in range(1, groups):
            source = lax.rem(grp + groups - k, groups)
            sel = jnp.where(partner == source, grp_land[par, k - 1], sel)
        sel_buf[...] = sel
        for k in range(1, n):
            gath_copy(k, me).start()
        gath[me] = sel

        for d in offs:

            @pl.when(jnp.logical_and(there(d), jnp.logical_not(last)))
            def _():
                halo_copy(par, d, -d).start()

        for k in range(1, n):
            gath_copy(k, lax.rem(me + n - k, n)).wait_recv()

        src = gath[...].reshape(n * tile, LANES)
        both = jnp.concatenate([jnp.where(q_of_row, 0.0, src), jnp.where(q_of_row, src, 0.0)], axis=1)
        hi, lo = split(both)
        lhs = jnp.concatenate([hi, lo], axis=0).T.astype(BF16)
        acc = jnp.zeros((n * tile, 4 * LANES), F32)
        for s0 in range(0, cap, group_of_slots):
            lanes = slice(s0 * LANES, s0 * LANES + width)
            slots = range(s0, s0 + group_of_slots)
            cent = jnp.concatenate([cent_ref[s : s + 1, :] for s in slots], axis=1) % LANES
            vals = dot_nn(lhs, oh_cent[:, lanes])
            hit = lane_of_chunk == cent
            cv = [
                jnp.sum(jnp.where(hit, vals[q * LANES : (q + 1) * LANES], 0.0), axis=0, keepdims=True)
                for q in range(2)
            ]
            hi, lo = split(jnp.concatenate(cv, axis=0))
            c4 = jnp.concatenate([hi, lo], axis=0).astype(BF16)
            contrib = []
            for i, s in enumerate(slots):
                r = dot_nt(c4[:, i * LANES : (i + 1) * LANES], maps2[s])
                r = r[:, :LANES] + r[:, LANES:]
                contrib.append(r[0:2] + r[2:4])
            hi, lo = split(jnp.concatenate(contrib, axis=1))
            targ = jnp.concatenate([targ_ref[s : s + 1, :] for s in slots], axis=1) % LANES
            hit = lane_of_chunk == targ
            rhs = jnp.concatenate(
                [jnp.where(hit, x[q : q + 1], 0.0).astype(BF16) for q in range(2) for x in (hi, lo)], axis=0
            )
            acc = acc + dot_nt(oh_targ[:, lanes], rhs)
        p0 = acc[:, :LANES] + acc[:, LANES : 2 * LANES]
        p1 = acc[:, 2 * LANES : 3 * LANES] + acc[:, 3 * LANES :]
        part[...] = jnp.where(q_of_row, p1, p0).reshape(n, tile, LANES)
        for k in range(1, n):
            rs_copy(k, me).start()

        @pl.when(first)
        def _():
            each(offs, lambda d: starts(rest_copies(d, (2,))))

        rs_land[me] = part[me]
        for k in range(1, n):
            rs_copy(k, lax.rem(me + n - k, n)).wait_recv()
        iface = rs_land[0]
        for j in range(1, n):
            iface = iface + rs_land[j]
        for q in range(2):
            for i in range(half):
                iface_ref[0, q : q + 1, i * LANES : (i + 1) * LANES] = iface[q * half + i : q * half + i + 1, :]
        inc = gain_t * (iface - exp_buf[...]) + pltpu.roll(gain_f * iface, half, 0)
        inc_buf[...] = inc
        for d in offs:

            @pl.when(jnp.logical_and(there(d), jnp.logical_not(last)))
            def _():
                inc_copy(d, -d).start()
                halo_copy(par, d, -d).wait_send()

        @pl.when(first)
        def _():
            each(offs, lambda d: arrivals(surf_copies(-d)))
            for d in offs:
                hot_rows(d + reach)

        fa[own] = final[own] + spread(reach, inc)

        @pl.when(first)
        def _():
            each(offs, lambda d: arrivals(rest_copies(-d, (0, 1, 2))))
            each(offs, lambda d: departures(rest_copies(d, (0, 1, 2)) + surf_copies(d)))

        @pl.when(jnp.logical_not(last))
        def _():
            for d in offs:

                @pl.when(there(d))
                def _():
                    halo_copy(par, -d, d).wait_recv()
                    inc_copy(-d, d).wait_recv()

                fa[pl.ds(depth + planes * d, planes)] = land[par, at[d]] + spread(d + reach, inc_land[at[d]])
            for d in offs:

                @pl.when(there(d))
                def _():
                    inc_copy(d, -d).wait_send()

        for k in range(1, groups):
            grp_copy(par, k).wait_send()
        for k in range(1, n):
            gath_copy(k, me).wait_send()
            rs_copy(k, me).wait_send()
        return carry

    pair = (fa, fb)
    each(beside, lambda d: arrivals(first_copies(-d)))
    each(beside, lambda d: departures(first_copies(d)))
    for k in range(near):
        step(pair[k % 2], pair[(k + 1) % 2], depth - near + k)
    each(beside, lambda d: mid_copy(d).start())
    each(offs, lambda d: starts(surf_copies(d) + rest_copies(d, (0, 1))))
    each(beside, lambda d: mid_copy(-d).wait_recv())
    for d in beside:
        fa[pl.ds(depth + planes * d, planes)] = land[1, at[d]]
    each(beside, lambda d: mid_copy(d).wait_send())
    for k in range(near):
        step(pair[k % 2], pair[(k + 1) % 2], depth - near + k)

    lax.fori_loop(0, COUPLE, couple, 0)

    def fold(b, carry):
        chunk = pl.ds(pl.multiple_of(b * 8 * LANES, LANES), 8 * LANES)
        rws = []
        for p in range(planes):
            x = fa[depth + p, pl.ds(pl.multiple_of(b * 8, 8), 8), :]
            rws.append(jnp.concatenate([x[i : i + 1, :] for i in range(8)], axis=1))
        out_ref[0, :, chunk] = jnp.concatenate(rws, axis=0)
        return carry

    lax.fori_loop(0, rows // 8, fold, 0)


def local_of(n, groups):
    def local(
        initial_field,
        conduct,
        velocity,
        heat_release,
        group_kind,
        partner,
        surface_cell,
        patch_count,
        patch_centres,
        patch_targets,
        patch_maps,
    ):
        _, planes, cells = initial_field.shape
        rows = cells // LANES
        surf_here = surface_cell.shape[1]
        cap = patch_centres.shape[1]
        reach = -(-STEPS // planes)
        ext = planes + 2 * reach * planes
        tile = 2 * surf_here // LANES
        vmem = pl.BlockSpec(memory_space=pltpu.VMEM)
        smem = pl.BlockSpec(memory_space=pltpu.SMEM)
        dma = pltpu.SemaphoreType.DMA
        nd = 2 * reach
        scratch = [
            pltpu.VMEM((ext, rows, LANES), F32),
            pltpu.VMEM((ext, rows, LANES), F32),
            pltpu.VMEM((ext, rows, LANES), F32),
            pltpu.VMEM((ext, rows, LANES), F32),
            pltpu.VMEM((ext, rows, LANES), F32),
            pltpu.VMEM((2, nd, planes, rows, LANES), F32),
            pltpu.VMEM((nd + 1, 1, surf_here), jnp.int32),
            pltpu.VMEM((nd + 1, planes * rows, surf_here), BF16),
            pltpu.VMEM((2 * n * tile, cap * LANES), BF16),
            pltpu.VMEM((n * tile, cap * LANES), BF16),
            pltpu.VMEM((cap, 2 * LANES, LANES), BF16),
            pltpu.VMEM((tile, LANES), F32),
            pltpu.VMEM((2, groups - 1, tile, LANES), F32),
            pltpu.VMEM((tile, LANES), F32),
            pltpu.VMEM((n, tile, LANES), F32),
            pltpu.VMEM((n, tile, LANES), F32),
            pltpu.VMEM((n, tile, LANES), F32),
            pltpu.VMEM((tile, LANES), F32),
            pltpu.VMEM((nd, tile, LANES), F32),
            dma((9, nd)),
            dma((9, nd)),
            dma((2, groups - 1)),
            dma((2, groups - 1)),
            dma((n - 1,)),
            dma((n - 1,)),
            dma((n - 1,)),
            dma((n - 1,)),
            dma((nd,)),
            dma((nd,)),
            dma((2, nd)),
            dma((2, nd)),
            pltpu.VMEM((cap, LANES, LANES), F32),
            dma(()),
        ]

        def body(*refs):
            kernel(n, groups, *refs)

        field, iface = pl.pallas_call(
            body,
            name="coupled",
            out_shape=(
                jax.ShapeDtypeStruct(initial_field.shape, F32),
                jax.ShapeDtypeStruct((1, 2, surf_here), F32),
            ),
            in_specs=[smem] * 3 + [vmem] * 7 + [pl.BlockSpec(memory_space=pl.ANY)],
            out_specs=(vmem, vmem),
            scratch_shapes=scratch,
            compiler_params=pltpu.CompilerParams(
                collective_id=0, has_side_effects=True, vmem_limit_bytes=56 * 1024 * 1024
            ),
        )(
            group_kind,
            partner,
            patch_count,
            initial_field,
            conduct,
            velocity,
            heat_release,
            surface_cell,
            patch_centres[0],
            patch_targets[0],
            patch_maps[0],
        )
        return field, iface

    return local


def solution(mesh):
    placed = (
        P("grp", "sub", None),
        P("grp", "sub", None),
        P("grp", "sub", None),
        P("grp", "sub", None),
        P(),
        P(),
        P("grp", "sub"),
        P("grp", None),
        P("grp", "sub", None),
        P("grp", "sub", None),
        P("grp", "sub", None, None),
    )
    return jax.shard_map(
        local_of(mesh.shape["sub"], mesh.shape["grp"]),
        mesh=mesh,
        in_specs=placed,
        out_specs=(P("grp", "sub", None), P("grp", None, "sub")),
        check_vma=False,
    )
```

profile of v0, /device:TPU:0, one launch (start us, length us, event | category | flops | bytes accessed | tf_op | source)
XLA Modules:
  0.0 92.7 jit_solution(12959443832614185185)
XLA Ops:
  0.6 89.2 %coupled.1 = (f32[1,2,16384]{2,1,0:T(2,128)}, f32[1,2,512]{2,1,0:T(2,128)}) custom-call(s32[4]{0:T(128)} %refs_0_.1, s32[4]{0:T(128)} %refs_1_.1, s32[1,8]{1,0:T(1,128)} %refs_2_.1, f32[1,2,16384]{2,1,0:T(2,128)} %refs_3_.1, f32[1,2,16384]{2,1,0:T(2,128)} %refs_4_.1, f32[1,2,16384]{2,1,0:T(2,128)} %refs_5_.1, f32[1,2,16384]{2,1,0:T(2,128)} %refs_6_.1, ...), custom_call_target="tpu_custom_call" | custom-call | tf_op jit(solution)/shard_map/coupled/pallas_call | solution.py:547
  89.8 1.6 %copy.15 = f32[1,2,16384]{2,1,0:T(2,128)} copy(f32[1,2,16384]{2,1,0:T(2,128)} %get-tuple-element.4) | data formatting | bytes 262144
  91.4 1.3 %copy.16 = f32[1,2,512]{2,1,0:T(2,128)} copy(f32[1,2,512]{2,1,0:T(2,128)} %get-tuple-element.5) | data formatting | bytes 8192
where the time goes:
time: 92.9 us; the launch traced here: 92.7 us
  Pallas kernels  89.2 us (96%)
  local copies, waits for them, and re-layouts  2.85 us (3%)
    pallas_call x1, Pallas kernels, local(): pl.pallas_call(body, name='coupled', out_shape=(jax.ShapeDtypeStruct(init...  89.2 us
    unnamed x2, local copies, waits for them, and re-layouts  2.85 us

commit v1 on v0

v1 whole, which is shorter than its diff:
```python
import jax
import jax.numpy as jnp
from jax import lax
from jax.experimental import pallas as pl
from jax.experimental.pallas import tpu as pltpu
from jax.sharding import PartitionSpec as P

STEPS = 4
COUPLE = 4
LANES = 128
F32 = jnp.float32
BF16 = jnp.bfloat16


def split(x):
    hi = x.astype(BF16).astype(F32)
    return hi, x - hi


def dot_nt(a, b):
    return lax.dot_general(a, b, (((1,), (1,)), ((), ())), preferred_element_type=F32)


def dot_nn(a, b):
    return lax.dot_general(a, b, (((1,), (0,)), ((), ())), preferred_element_type=F32)


def iota(shape, dim):
    return lax.broadcasted_iota(jnp.int32, shape, dim)


def in_plane(c):
    rows, cols = c.shape
    return (
        pltpu.roll(c, 1, 0)
        + pltpu.roll(c, rows - 1, 0)
        + pltpu.roll(c, 1, 1)
        + pltpu.roll(c, cols - 1, 1)
    )


def kernel(
    n,
    groups,
    kind_ref,
    partner_ref,
    count_ref,
    field_ref,
    cond_ref,
    vel_ref,
    heat_ref,
    surf_ref,
    cent_ref,
    targ_ref,
    maps_ref,
    out_ref,
    iface_ref,
    fa,
    fb,
    cx,
    vx,
    hx,
    land,
    surf_all,
    oh_surf,
    hot_surf,
    oh_lane,
    oh_cent,
    oh_targ,
    hot_targ,
    maps2,
    exp_one,
    exp_two,
    own_temp,
    land_one,
    land_two,
    part_one,
    part_two,
    rs_one,
    rs_two,
    set_send,
    set_recv,
    ex_send,
    ex_recv,
    rs_send,
    rs_recv,
    halo_send,
    halo_recv,
    maps,
    load_sem,
):
    planes = field_ref.shape[1]
    rows = fa.shape[1]
    near = STEPS // 2
    assert near % 2 == 0 and near <= planes
    surf_here = surf_ref.shape[1]
    cap = cent_ref.shape[0]
    reach = -(-STEPS // planes)
    depth = reach * planes
    ext = planes + 2 * depth
    offs = [d for d in range(-reach, reach + 1) if d != 0]
    at = {d: i for i, d in enumerate(offs)}
    half = surf_here // LANES
    span = 2 * reach + 1
    blocks = n * half
    me = lax.axis_index("sub")
    grp = lax.axis_index("grp")

    def there(d):
        return jnp.logical_and(me + d >= 0, me + d < n)

    def rcopy(src, dst, ss, rs, dev):
        return pltpu.make_async_remote_copy(
            src_ref=src,
            dst_ref=dst,
            send_sem=ss,
            recv_sem=rs,
            device_id=dev,
            device_id_type=pl.DeviceIdType.MESH,
        )

    load = pltpu.make_async_copy(maps_ref, maps, load_sem)
    load.start()

    for buf in (fa, cx, vx, hx):
        buf[...] = jnp.zeros(buf.shape, F32)
    land[...] = jnp.zeros(land.shape, F32)
    part_one[...] = jnp.zeros(part_one.shape, F32)
    surf_all[...] = jnp.zeros(surf_all.shape, jnp.int32)

    barrier = pltpu.get_barrier_semaphore()
    for k in range(1, n):
        pl.semaphore_signal(
            barrier, inc=1, device_id={"sub": lax.rem(me + k, n)}, device_id_type=pl.DeviceIdType.MESH
        )
    for k in range(1, groups):
        for j in range(n):
            pl.semaphore_signal(
                barrier,
                inc=1,
                device_id={"grp": lax.rem(grp + k, groups), "sub": lax.rem(me + j, n)},
                device_id_type=pl.DeviceIdType.MESH,
            )

    own = pl.ds(depth, planes)
    kind = kind_ref[grp]
    gas = jnp.where(kind == 0, 1.0, 0.0).astype(F32)
    gain_t = jnp.where(kind == 0, 0.5, 0.25).astype(F32)
    gain_f = jnp.where(kind == 0, -0.25, 0.25).astype(F32)
    away_t = jnp.where(kind == 0, 0.25, 0.5).astype(F32)
    away_f = jnp.where(kind == 0, 0.25, -0.25).astype(F32)
    fetch = ((field_ref, fa, None), (cond_ref, cx, None), (vel_ref, vx, gas), (heat_ref, hx, 0.5 * gas))

    def unfold(b, carry):
        chunk = pl.ds(pl.multiple_of(b * 8 * LANES, LANES), 8 * LANES)
        for src, dst, scale in fetch:
            x = src[0, :, chunk]
            if scale is not None:
                x = x * scale
            for p in range(planes):
                dst[depth + p, pl.ds(pl.multiple_of(b * 8, 8), 8), :] = jnp.concatenate(
                    [x[p : p + 1, i * LANES : (i + 1) * LANES] for i in range(8)], axis=0
                )
        return carry

    lax.fori_loop(0, rows // 8, unfold, 0)
    pl.semaphore_wait(barrier, n * groups - 1)

    def send_planes(buf, lo, hi, to, j):
        slot = -to
        shift = depth - (depth + planes * slot)
        return rcopy(
            buf.at[pl.ds(lo + shift, hi - lo)],
            buf.at[pl.ds(lo, hi - lo)],
            set_send.at[j, at[to]],
            set_recv.at[j, at[slot]],
            {"sub": me + to},
        )

    def first_copies(to):
        base = depth - planes * to
        lo, hi = max(base, depth - near), min(base + planes, depth + planes + near)
        out = [send_planes(fa, lo, hi, to, 0)]
        lo, hi = max(base, depth - near + 1), min(base + planes, depth + planes + near - 1)
        if hi > lo:
            out += [send_planes(buf, lo, hi, to, j + 1) for j, buf in enumerate((cx, vx, hx))]
        return out

    def rest_copies(to, which):
        base = depth - planes * to
        lo, hi = max(base, 1), min(base + planes, ext - 1)
        if to == 1:
            hi = min(hi, depth - near + 1)
        if to == -1:
            lo = max(lo, depth + planes + near - 1)
        if hi <= lo:
            return []
        return [send_planes((cx, vx, hx)[j], lo, hi, to, j + 4) for j in which]

    def surf_copies(to):
        return [
            rcopy(
                surf_ref,
                surf_all.at[reach - to],
                set_send.at[7, at[to]],
                set_recv.at[7, at[-to]],
                {"sub": me + to},
            )
        ]

    def mid_copy(to):
        return rcopy(
            fa.at[own],
            land.at[1, at[-to]],
            set_send.at[8, at[to]],
            set_recv.at[8, at[-to]],
            {"sub": me + to},
        )

    def each(ds, act):
        for d in ds:

            @pl.when(there(d))
            def _():
                act(d)

    def starts(copies):
        for c in copies:
            c.start()

    def arrivals(copies):
        for c in copies:
            c.wait_recv()

    def departures(copies):
        for c in copies:
            c.wait_send()

    beside = (-1, 1)
    each(beside, lambda d: starts(first_copies(d)))

    partner = partner_ref[grp]
    count = count_ref[0, me]
    surf_all[reach] = surf_ref[...]
    block_row = iota((blocks, LANES), 0)
    lane_row = iota((LANES, LANES), 0)

    def hot(mask):
        return jnp.where(mask, 1.0, 0.0).astype(F32)

    load.wait()
    for s in range(cap):
        lanes = pl.ds(s * LANES, LANES)
        oh_cent[:, lanes] = hot(lane_row == cent_ref[s : s + 1, :] % LANES).astype(BF16)
        oh_targ[:, lanes] = hot(block_row == targ_ref[s : s + 1, :] // LANES).astype(BF16)
        hot_targ[lanes, :] = hot(lane_row == targ_ref[s : s + 1, :] % LANES).T.astype(BF16)
        live = jnp.where(s < count, 1.0, 0.0).astype(F32)
        hi, lo = split((maps[s] * live).T)
        maps2[s, :, pl.ds(0, LANES)] = hi.astype(BF16)
        maps2[s, :, pl.ds(LANES, LANES)] = lo.astype(BF16)

    cell_row = iota((planes * rows, surf_here), 0)

    def hot_rows(j):
        oh_surf[j] = hot(cell_row == surf_all[j] // LANES).astype(BF16)
        lane = surf_all[j] % LANES
        for i in range(half):
            cols = slice(i * LANES, (i + 1) * LANES)
            hot_surf[j, cols, :] = hot(lane_row == lane[:, cols]).T.astype(BF16)

    hot_rows(reach)
    own_lane = hot(iota((LANES, surf_here), 0) == surf_all[reach] % LANES).astype(BF16)
    oh_lane[pl.ds(0, LANES)] = own_lane
    oh_lane[pl.ds(LANES, LANES)] = own_lane

    group_of_slots = 4 if cap % 4 == 0 else 1
    width = group_of_slots * LANES
    block_of_chunk = iota((blocks, width), 0)

    def step(src, dst, k):
        for z in range(k + 1, ext - k - 1):
            c = src[z]
            dn = src[z - 1]
            lap = src[z + 1] + dn + in_plane(c) - 6.0 * c
            dst[z] = c + cx[z] * lap - vx[z] * (c - dn) + hx[z] * (1.0 + jnp.tanh(c))

    def spread(slot, inc):
        packed = []
        for x in split(inc):
            wide = [jnp.broadcast_to(x[i : i + 1, :], (16, LANES)).astype(BF16) for i in range(half)]
            packed.append(jnp.concatenate(wide, axis=1))
        out = None
        for x in packed:
            lhs = jnp.concatenate(
                [oh_surf[slot, r * 16 : (r + 1) * 16, :] * x for r in range(planes * rows // 16)], axis=0
            )
            r = dot_nn(lhs, hot_surf[slot])
            out = r if out is None else out + r
        return out.reshape(planes, rows, LANES)

    def halo_copy(par, to, slot):
        return rcopy(
            fa.at[own],
            land.at[par, at[slot]],
            halo_send.at[par, at[to]],
            halo_recv.at[par, at[slot]],
            {"sub": me + to},
        )

    def ex_copy(two, par, k, j, sender):
        src, dst = (exp_two, land_two.at[k - 1, sender]) if two else (exp_one, land_one.at[par, k - 1, sender])
        return rcopy(
            src,
            dst,
            ex_send.at[par, k - 1, j],
            ex_recv.at[par, k - 1, j],
            {"grp": lax.rem(grp + k, groups), "sub": lax.rem(me + j, n)},
        )

    def rs_copy(two, par, k, sender):
        peer = lax.rem(me + k, n)
        if two:
            src, dst = part_two.at[peer], rs_two.at[sender]
        else:
            src, dst = part_one.at[pl.ds(peer, span)], rs_one.at[par, sender]
        return rcopy(src, dst, rs_send.at[par, k - 1], rs_recv.at[par, k - 1], {"sub": peer})

    def sample(values):
        lhs = []
        for x in values:
            hi, lo = split(jnp.concatenate(x, axis=0))
            lhs.append(jnp.concatenate([hi, lo], axis=1).astype(BF16))
        got = dot_nn(jnp.concatenate(lhs, axis=0), oh_lane[...])
        hit = cell_row == surf_all[reach] // LANES
        size = planes * rows
        return [
            jnp.sum(jnp.where(hit, got[q * size : (q + 1) * size], 0.0), axis=0, keepdims=True)
            for q in range(len(values))
        ]

    def patches(srcs):
        count_q = len(srcs)
        lhs = jnp.concatenate([x for v in srcs for x in split(v)], axis=0).astype(BF16)
        acc = None
        for s0 in range(0, cap, group_of_slots):
            lanes = slice(s0 * LANES, s0 * LANES + width)
            slots = range(s0, s0 + group_of_slots)
            cent = jnp.concatenate([cent_ref[s : s + 1, :] for s in slots], axis=1) // LANES
            vals = dot_nn(lhs, oh_cent[:, lanes])
            hit = block_of_chunk == cent
            cv = []
            for q in range(count_q):
                v = vals[2 * q * blocks : (2 * q + 1) * blocks] + vals[(2 * q + 1) * blocks : (2 * q + 2) * blocks]
                cv.append(jnp.sum(jnp.where(hit, v, 0.0), axis=0, keepdims=True))
            c4 = jnp.concatenate([x for v in cv for x in split(v)], axis=0).astype(BF16)
            contrib = []
            for i, s in enumerate(slots):
                r = dot_nn(c4[:, i * LANES : (i + 1) * LANES], maps2[s])
                contrib.append(r[:, :LANES] + r[:, LANES:])
            r = jnp.concatenate(contrib, axis=1)
            rows_of = []
            for q in range(count_q):
                for x in split(r[2 * q : 2 * q + 1] + r[2 * q + 1 : 2 * q + 2]):
                    wide = jnp.broadcast_to(x, (16, width)).astype(BF16)
                    rows_of += [oh_targ[b * 16 : (b + 1) * 16, lanes] * wide for b in range(blocks // 16)]
            r = dot_nn(jnp.concatenate(rows_of, axis=0), hot_targ[lanes, :])
            acc = r if acc is None else acc + r
        return [
            acc[2 * q * blocks : (2 * q + 1) * blocks] + acc[(2 * q + 1) * blocks : (2 * q + 2) * blocks]
            for q in range(count_q)
        ]

    def advance():
        for k in range(STEPS):
            step(pair[k % 2], pair[(k + 1) % 2], k)

    def surface():
        temp = [fa[depth + p] for p in range(planes)]
        flux = [cx[depth + p] * (4.0 * t - in_plane(t)) for p, t in enumerate(temp)]
        return temp, flux

    def exchange(two, par):
        for j in range(n - 1, -1, -1):
            for k in range(1, groups):
                ex_copy(two, par, k, j, me).start()

    def chosen(two, par):
        for j in range(n):
            for k in range(1, groups):
                ex_copy(two, par, k, j, lax.rem(me + n - j, n)).wait_recv()
        out = None
        for k in range(1, groups):
            got = land_two[k - 1] if two else land_one[par, k - 1]
            source = lax.rem(grp + groups - k, groups)
            out = got if out is None else jnp.where(partner == source, got, out)
        return out

    def finish(two, par):
        for j in range(n):
            for k in range(1, groups):
                ex_copy(two, par, k, j, me).wait_send()
        for k in range(1, n):
            rs_copy(two, par, k, me).wait_send()

    def couple(it, carry):
        par = lax.rem(it, 2)
        first = it == 0

        @pl.when(jnp.logical_not(first))
        def _():
            advance()

        temp, flux = surface()
        mixed = sample([[away_t * t + away_f * f for t, f in zip(temp, flux)]])[0]
        for i in range(half):
            exp_one[i : i + 1, :] = mixed[:, i * LANES : (i + 1) * LANES]
        exchange(False, par)
        for d in offs:

            @pl.when(there(d))
            def _():
                halo_copy(par, d, -d).start()

        here = sample([temp])[0]
        for i in range(half):
            own_temp[i : i + 1, :] = here[:, i * LANES : (i + 1) * LANES]

        srcs = chosen(False, par)
        part = patches([srcs.reshape(blocks, LANES)])[0].reshape(n, half, LANES)
        mine = iota((n, half, LANES), 0) == me
        part_one[pl.ds(reach, n)] = part - jnp.where(mine, gain_t * own_temp[...], 0.0)
        for k in range(1, n):
            rs_copy(False, par, k, me).start()

        @pl.when(first)
        def _():
            each(offs, lambda d: starts(rest_copies(d, (2,))))

        rs_one[par, me] = part_one[pl.ds(me, span)]

        @pl.when(first)
        def _():
            each(offs, lambda d: arrivals(surf_copies(-d)))
            for d in offs:
                hot_rows(d + reach)

        for d in offs:

            @pl.when(there(d))
            def _():
                halo_copy(par, d, -d).wait_send()
                halo_copy(par, -d, d).wait_recv()

        for k in range(1, n):
            rs_copy(False, par, k, lax.rem(me + n - k, n)).wait_recv()
        inc = rs_one[par, 0]
        for j in range(1, n):
            inc = inc + rs_one[par, j]
        fa[own] = fa[own] + spread(reach, inc[reach])
        for d in offs:
            fa[pl.ds(depth + planes * d, planes)] = land[par, at[d]] + spread(d + reach, inc[d + reach])

        @pl.when(first)
        def _():
            each(offs, lambda d: arrivals(rest_copies(-d, (0, 1, 2))))
            each(offs, lambda d: departures(rest_copies(d, (0, 1, 2)) + surf_copies(d)))

        finish(False, par)
        return carry

    def final():
        par = (COUPLE - 1) % 2
        advance()
        got = sample(surface())
        for q in range(2):
            for i in range(half):
                exp_two[q * half + i : q * half + i + 1, :] = got[q][:, i * LANES : (i + 1) * LANES]
        exchange(True, par)
        src = chosen(True, par)
        parts = patches([src[:, q * half : (q + 1) * half].reshape(blocks, LANES) for q in range(2)])
        part_two[...] = jnp.concatenate([x.reshape(n, half, LANES) for x in parts], axis=1)
        for k in range(1, n):
            rs_copy(True, par, k, me).start()
        rs_two[me] = part_two[me]
        for k in range(1, n):
            rs_copy(True, par, k, lax.rem(me + n - k, n)).wait_recv()
        iface = rs_two[0]
        for j in range(1, n):
            iface = iface + rs_two[j]
        for q in range(2):
            for i in range(half):
                iface_ref[0, q : q + 1, i * LANES : (i + 1) * LANES] = iface[q * half + i : q * half + i + 1, :]
        inc = gain_t * (iface[:half] - exp_two[:half]) + gain_f * iface[half:]
        fa[own] = fa[own] + spread(reach, inc)
        finish(True, par)

    pair = (fa, fb)
    each(beside, lambda d: arrivals(first_copies(-d)))
    each(beside, lambda d: departures(first_copies(d)))
    for k in range(near):
        step(pair[k % 2], pair[(k + 1) % 2], depth - near + k)
    each(beside, lambda d: mid_copy(d).start())
    each(offs, lambda d: starts(surf_copies(d) + rest_copies(d, (0, 1))))
    each(beside, lambda d: mid_copy(-d).wait_recv())
    for d in beside:
        fa[pl.ds(depth + planes * d, planes)] = land[1, at[d]]
    each(beside, lambda d: mid_copy(d).wait_send())
    for k in range(near):
        step(pair[k % 2], pair[(k + 1) % 2], depth - near + k)

    lax.fori_loop(0, COUPLE - 1, couple, 0)
    final()

    def fold(b, carry):
        chunk = pl.ds(pl.multiple_of(b * 8 * LANES, LANES), 8 * LANES)
        rws = []
        for p in range(planes):
            x = fa[depth + p, pl.ds(pl.multiple_of(b * 8, 8), 8), :]
            rws.append(jnp.concatenate([x[i : i + 1, :] for i in range(8)], axis=1))
        out_ref[0, :, chunk] = jnp.concatenate(rws, axis=0)
        return carry

    lax.fori_loop(0, rows // 8, fold, 0)


def local_of(n, groups):
    def local(
        initial_field,
        conduct,
        velocity,
        heat_release,
        group_kind,
        partner,
        surface_cell,
        patch_count,
        patch_centres,
        patch_targets,
        patch_maps,
    ):
        _, planes, cells = initial_field.shape
        rows = cells // LANES
        surf_here = surface_cell.shape[1]
        cap = patch_centres.shape[1]
        reach = -(-STEPS // planes)
        ext = planes + 2 * reach * planes
        half = surf_here // LANES
        vmem = pl.BlockSpec(memory_space=pltpu.VMEM)
        smem = pl.BlockSpec(memory_space=pltpu.SMEM)
        dma = pltpu.SemaphoreType.DMA
        nd = 2 * reach
        scratch = [
            pltpu.VMEM((ext, rows, LANES), F32),
            pltpu.VMEM((ext, rows, LANES), F32),
            pltpu.VMEM((ext, rows, LANES), F32),
            pltpu.VMEM((ext, rows, LANES), F32),
            pltpu.VMEM((ext, rows, LANES), F32),
            pltpu.VMEM((2, nd, planes, rows, LANES), F32),
            pltpu.VMEM((nd + 1, 1, surf_here), jnp.int32),
            pltpu.VMEM((nd + 1, planes * rows, surf_here), BF16),
            pltpu.VMEM((nd + 1, surf_here, LANES), BF16),
            pltpu.VMEM((2 * LANES, surf_here), BF16),
            pltpu.VMEM((LANES, cap * LANES), BF16),
            pltpu.VMEM((n * half, cap * LANES), BF16),
            pltpu.VMEM((cap * LANES, LANES), BF16),
            pltpu.VMEM((cap, LANES, 2 * LANES), BF16),
            pltpu.VMEM((half, LANES), F32),
            pltpu.VMEM((2 * half, LANES), F32),
            pltpu.VMEM((half, LANES), F32),
            pltpu.VMEM((2, groups - 1, n, half, LANES), F32),
            pltpu.VMEM((groups - 1, n, 2 * half, LANES), F32),
            pltpu.VMEM((n + nd, half, LANES), F32),
            pltpu.VMEM((n, 2 * half, LANES), F32),
            pltpu.VMEM((2, n, nd + 1, half, LANES), F32),
            pltpu.VMEM((n, 2 * half, LANES), F32),
            dma((9, nd)),
            dma((9, nd)),
            dma((2, groups - 1, n)),
            dma((2, groups - 1, n)),
            dma((2, n - 1)),
            dma((2, n - 1)),
            dma((2, nd)),
            dma((2, nd)),
            pltpu.VMEM((cap, LANES, LANES), F32),
            dma(()),
        ]

        def body(*refs):
            kernel(n, groups, *refs)

        field, iface = pl.pallas_call(
            body,
            name="coupled",
            out_shape=(
                jax.ShapeDtypeStruct(initial_field.shape, F32),
                jax.ShapeDtypeStruct((1, 2, surf_here), F32),
            ),
            in_specs=[smem] * 3 + [vmem] * 7 + [pl.BlockSpec(memory_space=pl.ANY)],
            out_specs=(vmem, vmem),
            scratch_shapes=scratch,
            compiler_params=pltpu.CompilerParams(
                collective_id=0, has_side_effects=True, vmem_limit_bytes=56 * 1024 * 1024
            ),
        )(
            group_kind,
            partner,
            patch_count,
            initial_field,
            conduct,
            velocity,
            heat_release,
            surface_cell,
            patch_centres[0],
            patch_targets[0],
            patch_maps[0],
        )
        return field, iface

    return local


def solution(mesh):
    placed = (
        P("grp", "sub", None),
        P("grp", "sub", None),
        P("grp", "sub", None),
        P("grp", "sub", None),
        P(),
        P(),
        P("grp", "sub"),
        P("grp", None),
        P("grp", "sub", None),
        P("grp", "sub", None),
        P("grp", "sub", None, None),
    )
    return jax.shard_map(
        local_of(mesh.shape["sub"], mesh.shape["grp"]),
        mesh=mesh,
        in_specs=placed,
        out_specs=(P("grp", "sub", None), P("grp", None, "sub")),
        check_vma=False,
    )
```

time: 92.9 us -> 76.7 us (0.83)
  Pallas kernels: 89.2 us -> 73 us
    pallas_call x1, Pallas kernels: 89.2 us -> 73 us  [local(): pl.pallas_call(body, name='coupled', out_shape=(jax.ShapeDtypeStruct(init...]
where the time goes in v1:
time: 76.7 us; the launch traced here: 76.5 us
  Pallas kernels  73 us (95%)
  local copies, waits for them, and re-layouts  2.85 us (4%)
    pallas_call x1, Pallas kernels, local(): pl.pallas_call(body, name='coupled', out_shape=(jax.ShapeDtypeStruct(init...  73 us
    unnamed x2, local copies, waits for them, and re-layouts  2.85 us

profile of v1, /device:TPU:0, one launch (start us, length us, event | category | flops | bytes accessed | tf_op | source)
XLA Modules:
  0.0 76.5 jit_solution(345311170883490141)
XLA Ops:
  0.6 73.0 %coupled.1 = (f32[1,2,16384]{2,1,0:T(2,128)}, f32[1,2,512]{2,1,0:T(2,128)}) custom-call(s32[4]{0:T(128)} %refs_0_.1, s32[4]{0:T(128)} %refs_1_.1, s32[1,8]{1,0:T(1,128)} %refs_2_.1, f32[1,2,16384]{2,1,0:T(2,128)} %refs_3_.1, f32[1,2,16384]{2,1,0:T(2,128)} %refs_4_.1, f32[1,2,16384]{2,1,0:T(2,128)} %refs_5_.1, f32[1,2,16384]{2,1,0:T(2,128)} %refs_6_.1, ...), custom_call_target="tpu_custom_call" | custom-call | tf_op jit(solution)/shard_map/coupled/pallas_call | solution.py:590
  73.6 1.6 %copy.15 = f32[1,2,16384]{2,1,0:T(2,128)} copy(f32[1,2,16384]{2,1,0:T(2,128)} %get-tuple-element.4) | data formatting | bytes 262144
  75.2 1.3 %copy.16 = f32[1,2,512]{2,1,0:T(2,128)} copy(f32[1,2,512]{2,1,0:T(2,128)} %get-tuple-element.5) | data formatting | bytes 8192

commit v2 on v1

--- a/solution.py
+++ b/solution.py
@@ -259,19 +259,24 @@
         maps2[s, :, pl.ds(0, LANES)] = hi.astype(BF16)
         maps2[s, :, pl.ds(LANES, LANES)] = lo.astype(BF16)
 
-    cell_row = iota((planes * rows, surf_here), 0)
+    cell_row = iota((rows, surf_here), 0)
+
+    def row_of(cell):
+        return (cell // LANES) % rows
+
+    def spot_of(cell):
+        return cell // (rows * LANES) * LANES + cell % LANES
 
     def hot_rows(j):
-        oh_surf[j] = hot(cell_row == surf_all[j] // LANES).astype(BF16)
-        lane = surf_all[j] % LANES
+        oh_surf[j] = hot(cell_row == row_of(surf_all[j])).astype(BF16)
+        spot = spot_of(surf_all[j])
         for i in range(half):
             cols = slice(i * LANES, (i + 1) * LANES)
-            hot_surf[j, cols, :] = hot(lane_row == lane[:, cols]).T.astype(BF16)
+            for p in range(planes):
+                hot_surf[j, cols, pl.ds(p * LANES, LANES)] = hot(lane_row + p * LANES == spot[:, cols]).T.astype(BF16)
 
     hot_rows(reach)
-    own_lane = hot(iota((LANES, surf_here), 0) == surf_all[reach] % LANES).astype(BF16)
-    oh_lane[pl.ds(0, LANES)] = own_lane
-    oh_lane[pl.ds(LANES, LANES)] = own_lane
+    oh_lane[...] = hot(iota((planes * LANES, surf_here), 0) == spot_of(surf_all[reach])).astype(BF16)
 
     group_of_slots = 4 if cap % 4 == 0 else 1
     width = group_of_slots * LANES
@@ -285,18 +290,14 @@
             dst[z] = c + cx[z] * lap - vx[z] * (c - dn) + hx[z] * (1.0 + jnp.tanh(c))
 
     def spread(slot, inc):
-        packed = []
+        lhs = []
         for x in split(inc):
             wide = [jnp.broadcast_to(x[i : i + 1, :], (16, LANES)).astype(BF16) for i in range(half)]
-            packed.append(jnp.concatenate(wide, axis=1))
-        out = None
-        for x in packed:
-            lhs = jnp.concatenate(
-                [oh_surf[slot, r * 16 : (r + 1) * 16, :] * x for r in range(planes * rows // 16)], axis=0
-            )
-            r = dot_nn(lhs, hot_surf[slot])
-            out = r if out is None else out + r
-        return out.reshape(planes, rows, LANES)
+            wide = jnp.concatenate(wide, axis=1)
+            lhs += [oh_surf[slot, r * 16 : (r + 1) * 16, :] * wide for r in range(rows // 16)]
+        r = dot_nn(jnp.concatenate(lhs, axis=0), hot_surf[slot])
+        r = r[:rows] + r[rows:]
+        return [r[:, p * LANES : (p + 1) * LANES] for p in range(planes)]
 
     def halo_copy(par, to, slot):
         return rcopy(
@@ -307,14 +308,16 @@
             {"sub": me + to},
         )
 
-    def ex_copy(two, par, k, j, sender):
+    upper = 2 * me >= n
+
+    def ex_copy(two, par, k, peer, sender):
         src, dst = (exp_two, land_two.at[k - 1, sender]) if two else (exp_one, land_one.at[par, k - 1, sender])
         return rcopy(
             src,
             dst,
-            ex_send.at[par, k - 1, j],
-            ex_recv.at[par, k - 1, j],
-            {"grp": lax.rem(grp + k, groups), "sub": lax.rem(me + j, n)},
+            ex_send.at[par, k - 1, peer],
+            ex_recv.at[par, k - 1, sender],
+            {"grp": lax.rem(grp + k, groups), "sub": peer},
         )
 
     def rs_copy(two, par, k, sender):
@@ -328,15 +331,14 @@
     def sample(values):
         lhs = []
         for x in values:
-            hi, lo = split(jnp.concatenate(x, axis=0))
-            lhs.append(jnp.concatenate([hi, lo], axis=1).astype(BF16))
-        got = dot_nn(jnp.concatenate(lhs, axis=0), oh_lane[...])
-        hit = cell_row == surf_all[reach] // LANES
-        size = planes * rows
-        return [
-            jnp.sum(jnp.where(hit, got[q * size : (q + 1) * size], 0.0), axis=0, keepdims=True)
-            for q in range(len(values))
-        ]
+            lhs += split(jnp.concatenate(x, axis=1))
+        got = dot_nn(jnp.concatenate(lhs, axis=0).astype(BF16), oh_lane[...])
+        hit = cell_row == row_of(surf_all[reach])
+        out = []
+        for q in range(len(values)):
+            v = got[2 * q * rows : (2 * q + 1) * rows] + got[(2 * q + 1) * rows : (2 * q + 2) * rows]
+            out.append(jnp.sum(jnp.where(hit, v, 0.0), axis=0, keepdims=True))
+        return out
 
     def patches(srcs):
         count_q = len(srcs)
@@ -380,14 +382,15 @@
         return temp, flux
 
     def exchange(two, par):
-        for j in range(n - 1, -1, -1):
+        for j in range(n):
+            peer = jnp.where(upper, j, n - 1 - j)
             for k in range(1, groups):
-                ex_copy(two, par, k, j, me).start()
+                ex_copy(two, par, k, peer, me).start()
 
     def chosen(two, par):
         for j in range(n):
             for k in range(1, groups):
-                ex_copy(two, par, k, j, lax.rem(me + n - j, n)).wait_recv()
+                ex_copy(two, par, k, me, j).wait_recv()
         out = None
         for k in range(1, groups):
             got = land_two[k - 1] if two else land_one[par, k - 1]
@@ -456,9 +459,11 @@
         inc = rs_one[par, 0]
         for j in range(1, n):
             inc = inc + rs_one[par, j]
-        fa[own] = fa[own] + spread(reach, inc[reach])
+        for p, x in enumerate(spread(reach, inc[reach])):
+            fa[depth + p] = fa[depth + p] + x
         for d in offs:
-            fa[pl.ds(depth + planes * d, planes)] = land[par, at[d]] + spread(d + reach, inc[d + reach])
+            for p, x in enumerate(spread(d + reach, inc[d + reach])):
+                fa[depth + planes * d + p] = land[par, at[d], p] + x
 
         @pl.when(first)
         def _():
@@ -487,11 +492,10 @@
         iface = rs_two[0]
         for j in range(1, n):
             iface = iface + rs_two[j]
-        for q in range(2):
-            for i in range(half):
-                iface_ref[0, q : q + 1, i * LANES : (i + 1) * LANES] = iface[q * half + i : q * half + i + 1, :]
+        iface_ref[...] = iface
         inc = gain_t * (iface[:half] - exp_two[:half]) + gain_f * iface[half:]
-        fa[own] = fa[own] + spread(reach, inc)
+        for p, x in enumerate(spread(reach, inc)):
+            out_ref[p] = fa[depth + p] + x
         finish(True, par)
 
     pair = (fa, fb)
@@ -511,16 +515,19 @@
     lax.fori_loop(0, COUPLE - 1, couple, 0)
     final()
 
-    def fold(b, carry):
-        chunk = pl.ds(pl.multiple_of(b * 8 * LANES, LANES), 8 * LANES)
+
+def unpack(planes_ref, rows_ref, out_ref, iface_ref):
+    planes, rows, _ = planes_ref.shape
+    half = rows_ref.shape[0] // 2
+    for b in range(rows // 8):
         rws = []
         for p in range(planes):
-            x = fa[depth + p, pl.ds(pl.multiple_of(b * 8, 8), 8), :]
+            x = planes_ref[p, b * 8 : (b + 1) * 8, :]
             rws.append(jnp.concatenate([x[i : i + 1, :] for i in range(8)], axis=1))
-        out_ref[0, :, chunk] = jnp.concatenate(rws, axis=0)
-        return carry
-
-    lax.fori_loop(0, rows // 8, fold, 0)
+        out_ref[0, :, b * 8 * LANES : (b + 1) * 8 * LANES] = jnp.concatenate(rws, axis=0)
+    for q in range(2):
+        for i in range(half):
+            iface_ref[0, q : q + 1, i * LANES : (i + 1) * LANES] = rows_ref[q * half + i : q * half + i + 1, :]
 
 
 def local_of(n, groups):
@@ -556,9 +563,9 @@
             pltpu.VMEM((ext, rows, LANES), F32),
             pltpu.VMEM((2, nd, planes, rows, LANES), F32),
             pltpu.VMEM((nd + 1, 1, surf_here), jnp.int32),
-            pltpu.VMEM((nd + 1, planes * rows, surf_here), BF16),
-            pltpu.VMEM((nd + 1, surf_here, LANES), BF16),
-            pltpu.VMEM((2 * LANES, surf_here), BF16),
+            pltpu.VMEM((nd + 1, rows, surf_here), BF16),
+            pltpu.VMEM((nd + 1, surf_here, planes * LANES), BF16),
+            pltpu.VMEM((planes * LANES, surf_here), BF16),
             pltpu.VMEM((LANES, cap * LANES), BF16),
             pltpu.VMEM((n * half, cap * LANES), BF16),
             pltpu.VMEM((cap * LANES, LANES), BF16),
@@ -587,12 +594,12 @@
         def body(*refs):
             kernel(n, groups, *refs)
 
-        field, iface = pl.pallas_call(
+        lying, tops = pl.pallas_call(
             body,
             name="coupled",
             out_shape=(
-                jax.ShapeDtypeStruct(initial_field.shape, F32),
-                jax.ShapeDtypeStruct((1, 2, surf_here), F32),
+                pltpu.VMEM((planes, rows, LANES), F32),
+                pltpu.VMEM((2 * half, LANES), F32),
             ),
             in_specs=[smem] * 3 + [vmem] * 7 + [pl.BlockSpec(memory_space=pl.ANY)],
             out_specs=(vmem, vmem),
@@ -613,7 +620,16 @@
             patch_targets[0],
             patch_maps[0],
         )
-        return field, iface
+        return pl.pallas_call(
+            unpack,
+            name="unpack",
+            out_shape=(
+                jax.ShapeDtypeStruct(initial_field.shape, F32),
+                jax.ShapeDtypeStruct((1, 2, surf_here), F32),
+            ),
+            in_specs=[vmem] * 2,
+            out_specs=(vmem, vmem),
+        )(*(pltpu.with_memory_space_constraint(x, pltpu.VMEM) for x in (lying, tops)))
 
     return local
 

time: 76.7 us -> 72.3 us (0.943)
  local copies, waits for them, and re-layouts: 2.85 us -> 0 us
  Pallas kernels: 73 us -> 71.5 us
    unnamed x2 -> x0, local copies, waits for them, and re-layouts: 2.85 us -> none
    pallas_call x1 -> x2, Pallas kernels: 73 us -> 71.5 us  [the longest x1 70.7 us: local(): pl.pallas_call(body, name='coupled', out_shape=(pltpu.VMEM((planes, rows,...]
where the time goes in v2:
time: 72.3 us; the launch traced here: 72.1 us
  Pallas kernels  71.5 us (99%)
    pallas_call x1, Pallas kernels, local(): pl.pallas_call(body, name='coupled', out_shape=(pltpu.VMEM((planes, rows,...  70.7 us

profile of v2, /device:TPU:0, one launch (start us, length us, event | category | flops | bytes accessed | tf_op | source)
XLA Modules:
  0.0 72.1 jit_solution(14171607395488767042)
XLA Ops:
  0.6 70.7 %coupled.1 = (f32[2,128,128]{2,1,0:T(8,128)S(1)}, f32[8,128]{1,0:T(8,128)S(1)}) custom-call(s32[4]{0:T(128)} %refs_0_.1, s32[4]{0:T(128)} %refs_1_.1, s32[1,8]{1,0:T(1,128)} %refs_2_.1, f32[1,2,16384]{2,1,0:T(2,128)} %refs_3_.1, f32[1,2,16384]{2,1,0:T(2,128)} %refs_4_.1, f32[1,2,16384]{2,1,0:T(2,128)} %refs_5_.1, f32[1,2,16384]{2,1,0:T(2,128)} %refs_6_.1, ...), custom_call_target="tpu_custom_call" | custom-call | tf_op jit(solution)/shard_map/coupled/pallas_call | solution.py:597
  71.4 0.7 %unpack.1 = (f32[1,2,16384]{2,1,0:T(2,128)}, f32[1,2,512]{2,1,0:T(2,128)}) custom-call(f32[2,128,128]{2,1,0:T(8,128)S(1)} %get-tuple-element.4.planes_ref, f32[8,128]{1,0:T(8,128)S(1)} %get-tuple-element.5.rows_ref), custom_call_target="tpu_custom_call" | custom-call | tf_op jit(solution)/shard_map/unpack/pallas_call | solution.py:623

commit v3 on v2

--- a/solution.py
+++ b/solution.py
@@ -42,17 +42,17 @@
 def kernel(
     n,
     groups,
-    kind_ref,
-    partner_ref,
-    count_ref,
-    field_ref,
-    cond_ref,
-    vel_ref,
-    heat_ref,
-    surf_ref,
-    cent_ref,
-    targ_ref,
-    maps_ref,
+    kind_hbm,
+    partner_hbm,
+    count_hbm,
+    field_hbm,
+    cond_hbm,
+    vel_hbm,
+    heat_hbm,
+    surf_hbm,
+    cent_hbm,
+    targ_hbm,
+    maps_hbm,
     out_ref,
     iface_ref,
     fa,
@@ -86,14 +86,23 @@
     rs_recv,
     halo_send,
     halo_recv,
+    kind_ref,
+    partner_ref,
+    count_ref,
+    field_ref,
+    cond_ref,
+    vel_ref,
+    heat_ref,
+    cent_ref,
+    targ_ref,
     maps,
     load_sem,
 ):
-    planes = field_ref.shape[1]
+    planes = field_ref.shape[0]
     rows = fa.shape[1]
     near = STEPS // 2
     assert near % 2 == 0 and near <= planes
-    surf_here = surf_ref.shape[1]
+    surf_here = surf_all.shape[2]
     cap = cent_ref.shape[0]
     reach = -(-STEPS // planes)
     depth = reach * planes
@@ -119,14 +128,22 @@
             device_id_type=pl.DeviceIdType.MESH,
         )
 
-    load = pltpu.make_async_copy(maps_ref, maps, load_sem)
-    load.start()
-
-    for buf in (fa, cx, vx, hx):
-        buf[...] = jnp.zeros(buf.shape, F32)
-    land[...] = jnp.zeros(land.shape, F32)
-    part_one[...] = jnp.zeros(part_one.shape, F32)
-    surf_all[...] = jnp.zeros(surf_all.shape, jnp.int32)
+    pairs = (
+        (kind_hbm, kind_ref),
+        (partner_hbm, partner_ref),
+        (count_hbm, count_ref),
+        (field_hbm.at[0], field_ref),
+        (cond_hbm.at[0], cond_ref),
+        (vel_hbm.at[0], vel_ref),
+        (heat_hbm.at[0], heat_ref),
+        (surf_hbm, surf_all.at[reach]),
+        (cent_hbm, cent_ref),
+        (targ_hbm, targ_ref),
+        (maps_hbm, maps),
+    )
+    loads = [pltpu.make_async_copy(src, dst, load_sem.at[i]) for i, (src, dst) in enumerate(pairs)]
+    for c in loads:
+        c.start()
 
     barrier = pltpu.get_barrier_semaphore()
     for k in range(1, n):
@@ -142,6 +159,20 @@
                 device_id_type=pl.DeviceIdType.MESH,
             )
 
+    for border in (pl.ds(0, reach), pl.ds(reach + n, reach)):
+        part_one[border] = jnp.zeros((reach, half, LANES), F32)
+    for d in offs:
+
+        @pl.when(jnp.logical_not(there(d)))
+        def _():
+            for buf in (fa, cx, vx, hx):
+                buf[pl.ds(depth + planes * d, planes)] = jnp.zeros((planes, rows, LANES), F32)
+            for par in range(2):
+                land[par, at[d]] = jnp.zeros((planes, rows, LANES), F32)
+            surf_all[reach + d] = jnp.zeros((1, surf_here), jnp.int32)
+
+    for c in loads[:7]:
+        c.wait()
     own = pl.ds(depth, planes)
     kind = kind_ref[grp]
     gas = jnp.where(kind == 0, 1.0, 0.0).astype(F32)
@@ -154,7 +185,7 @@
     def unfold(b, carry):
         chunk = pl.ds(pl.multiple_of(b * 8 * LANES, LANES), 8 * LANES)
         for src, dst, scale in fetch:
-            x = src[0, :, chunk]
+            x = src[:, chunk]
             if scale is not None:
                 x = x * scale
             for p in range(planes):
@@ -200,7 +231,7 @@
     def surf_copies(to):
         return [
             rcopy(
-                surf_ref,
+                surf_all.at[reach],
                 surf_all.at[reach - to],
                 set_send.at[7, at[to]],
                 set_recv.at[7, at[-to]],
@@ -241,19 +272,25 @@
 
     partner = partner_ref[grp]
     count = count_ref[0, me]
-    surf_all[reach] = surf_ref[...]
     block_row = iota((blocks, LANES), 0)
     lane_row = iota((LANES, LANES), 0)
 
+    def block_of(x):
+        return lax.shift_right_logical(x, jnp.full(x.shape, LANES.bit_length() - 1, jnp.int32))
+
+    def lane_of(x):
+        return lax.bitwise_and(x, jnp.full(x.shape, LANES - 1, jnp.int32))
+
     def hot(mask):
         return jnp.where(mask, 1.0, 0.0).astype(F32)
 
-    load.wait()
+    for c in loads[7:]:
+        c.wait()
     for s in range(cap):
         lanes = pl.ds(s * LANES, LANES)
-        oh_cent[:, lanes] = hot(lane_row == cent_ref[s : s + 1, :] % LANES).astype(BF16)
-        oh_targ[:, lanes] = hot(block_row == targ_ref[s : s + 1, :] // LANES).astype(BF16)
-        hot_targ[lanes, :] = hot(lane_row == targ_ref[s : s + 1, :] % LANES).T.astype(BF16)
+        oh_cent[:, lanes] = hot(lane_row == lane_of(cent_ref[s : s + 1, :])).astype(BF16)
+        oh_targ[:, lanes] = hot(block_row == block_of(targ_ref[s : s + 1, :])).astype(BF16)
+        hot_targ[lanes, :] = hot(lane_row == lane_of(targ_ref[s : s + 1, :])).T.astype(BF16)
         live = jnp.where(s < count, 1.0, 0.0).astype(F32)
         hi, lo = split((maps[s] * live).T)
         maps2[s, :, pl.ds(0, LANES)] = hi.astype(BF16)
@@ -261,11 +298,14 @@
 
     cell_row = iota((rows, surf_here), 0)
 
+    def plane_of(cell):
+        return sum((cell >= p * rows * LANES).astype(jnp.int32) for p in range(1, planes))
+
     def row_of(cell):
-        return (cell // LANES) % rows
+        return block_of(cell) - plane_of(cell) * rows
 
     def spot_of(cell):
-        return cell // (rows * LANES) * LANES + cell % LANES
+        return plane_of(cell) * LANES + lane_of(cell)
 
     def hot_rows(j):
         oh_surf[j] = hot(cell_row == row_of(surf_all[j])).astype(BF16)
@@ -278,9 +318,7 @@
     hot_rows(reach)
     oh_lane[...] = hot(iota((planes * LANES, surf_here), 0) == spot_of(surf_all[reach])).astype(BF16)
 
-    group_of_slots = 4 if cap % 4 == 0 else 1
-    width = group_of_slots * LANES
-    block_of_chunk = iota((blocks, width), 0)
+    block_of_slot = iota((blocks, cap * LANES), 0)
 
     def step(src, dst, k):
         for z in range(k + 1, ext - k - 1):
@@ -343,30 +381,25 @@
     def patches(srcs):
         count_q = len(srcs)
         lhs = jnp.concatenate([x for v in srcs for x in split(v)], axis=0).astype(BF16)
-        acc = None
-        for s0 in range(0, cap, group_of_slots):
-            lanes = slice(s0 * LANES, s0 * LANES + width)
-            slots = range(s0, s0 + group_of_slots)
-            cent = jnp.concatenate([cent_ref[s : s + 1, :] for s in slots], axis=1) // LANES
-            vals = dot_nn(lhs, oh_cent[:, lanes])
-            hit = block_of_chunk == cent
-            cv = []
-            for q in range(count_q):
-                v = vals[2 * q * blocks : (2 * q + 1) * blocks] + vals[(2 * q + 1) * blocks : (2 * q + 2) * blocks]
-                cv.append(jnp.sum(jnp.where(hit, v, 0.0), axis=0, keepdims=True))
-            c4 = jnp.concatenate([x for v in cv for x in split(v)], axis=0).astype(BF16)
-            contrib = []
-            for i, s in enumerate(slots):
-                r = dot_nn(c4[:, i * LANES : (i + 1) * LANES], maps2[s])
-                contrib.append(r[:, :LANES] + r[:, LANES:])
-            r = jnp.concatenate(contrib, axis=1)
-            rows_of = []
-            for q in range(count_q):
-                for x in split(r[2 * q : 2 * q + 1] + r[2 * q + 1 : 2 * q + 2]):
-                    wide = jnp.broadcast_to(x, (16, width)).astype(BF16)
-                    rows_of += [oh_targ[b * 16 : (b + 1) * 16, lanes] * wide for b in range(blocks // 16)]
-            r = dot_nn(jnp.concatenate(rows_of, axis=0), hot_targ[lanes, :])
-            acc = r if acc is None else acc + r
+        vals = dot_nn(lhs, oh_cent[...])
+        cent = jnp.concatenate([cent_ref[s : s + 1, :] for s in range(cap)], axis=1)
+        hit = block_of_slot == block_of(cent)
+        cv = []
+        for q in range(count_q):
+            v = vals[2 * q * blocks : (2 * q + 1) * blocks] + vals[(2 * q + 1) * blocks : (2 * q + 2) * blocks]
+            cv.append(jnp.sum(jnp.where(hit, v, 0.0), axis=0, keepdims=True))
+        c4 = jnp.concatenate([x for v in cv for x in split(v)], axis=0).astype(BF16)
+        contrib = []
+        for s in range(cap):
+            r = dot_nn(c4[:, s * LANES : (s + 1) * LANES], maps2[s])
+            contrib.append(r[:, :LANES] + r[:, LANES:])
+        r = jnp.concatenate(contrib, axis=1)
+        rows_of = []
+        for q in range(count_q):
+            for x in split(r[2 * q : 2 * q + 1] + r[2 * q + 1 : 2 * q + 2]):
+                wide = jnp.broadcast_to(x, (16, cap * LANES)).astype(BF16)
+                rows_of += [oh_targ[b * 16 : (b + 1) * 16, :] * wide for b in range(blocks // 16)]
+        acc = dot_nn(jnp.concatenate(rows_of, axis=0), hot_targ[...])
         return [
             acc[2 * q * blocks : (2 * q + 1) * blocks] + acc[(2 * q + 1) * blocks : (2 * q + 2) * blocks]
             for q in range(count_q)
@@ -459,11 +492,12 @@
         inc = rs_one[par, 0]
         for j in range(1, n):
             inc = inc + rs_one[par, j]
-        for p, x in enumerate(spread(reach, inc[reach])):
-            fa[depth + p] = fa[depth + p] + x
+        sums = [spread(slot, inc[slot]) for slot in range(span)]
+        for p in range(planes):
+            fa[depth + p] = fa[depth + p] + sums[reach][p]
         for d in offs:
-            for p, x in enumerate(spread(d + reach, inc[d + reach])):
-                fa[depth + planes * d + p] = land[par, at[d], p] + x
+            for p in range(planes):
+                fa[depth + planes * d + p] = land[par, at[d], p] + sums[d + reach][p]
 
         @pl.when(first)
         def _():
@@ -552,7 +586,6 @@
         ext = planes + 2 * reach * planes
         half = surf_here // LANES
         vmem = pl.BlockSpec(memory_space=pltpu.VMEM)
-        smem = pl.BlockSpec(memory_space=pltpu.SMEM)
         dma = pltpu.SemaphoreType.DMA
         nd = 2 * reach
         scratch = [
@@ -587,8 +620,17 @@
             dma((2, n - 1)),
             dma((2, nd)),
             dma((2, nd)),
+            pltpu.SMEM(group_kind.shape, jnp.int32),
+            pltpu.SMEM(partner.shape, jnp.int32),
+            pltpu.SMEM(patch_count.shape, jnp.int32),
+            pltpu.VMEM((planes, cells), F32),
+            pltpu.VMEM((planes, cells), F32),
+            pltpu.VMEM((planes, cells), F32),
+            pltpu.VMEM((planes, cells), F32),
+            pltpu.VMEM((cap, LANES), jnp.int32),
+            pltpu.VMEM((cap, LANES), jnp.int32),
             pltpu.VMEM((cap, LANES, LANES), F32),
-            dma(()),
+            dma((11,)),
         ]
 
         def body(*refs):
@@ -601,7 +643,7 @@
                 pltpu.VMEM((planes, rows, LANES), F32),
                 pltpu.VMEM((2 * half, LANES), F32),
             ),
-            in_specs=[smem] * 3 + [vmem] * 7 + [pl.BlockSpec(memory_space=pl.ANY)],
+            in_specs=[pl.BlockSpec(memory_space=pltpu.HBM)] * 11,
             out_specs=(vmem, vmem),
             scratch_shapes=scratch,
             compiler_params=pltpu.CompilerParams(

time: 72.3 us -> 66.1 us (0.914)
  Pallas kernels: 71.5 us -> 65.3 us
    pallas_call x1, Pallas kernels: 70.7 us -> 64.6 us  [local(): pl.pallas_call(body, name='coupled', out_shape=(pltpu.VMEM((planes, rows,...]
where the time goes in v3:
time: 66.1 us; the launch traced here: 66 us
  Pallas kernels  65.3 us (99%)
    pallas_call x1, Pallas kernels, local(): pl.pallas_call(body, name='coupled', out_shape=(pltpu.VMEM((planes, rows,...  64.6 us

profile of v3, /device:TPU:0, one launch (start us, length us, event | category | flops | bytes accessed | tf_op | source)
XLA Modules:
  0.0 66.0 jit_solution(2670442739341962905)
XLA Ops:
  0.6 64.6 %coupled.1 = (f32[2,128,128]{2,1,0:T(8,128)S(1)}, f32[8,128]{1,0:T(8,128)S(1)}) custom-call(s32[4]{0:T(128)} %refs_0_.1, s32[4]{0:T(128)} %refs_1_.1, s32[1,8]{1,0:T(1,128)} %refs_2_.1, f32[1,2,16384]{2,1,0:T(2,128)} %refs_3_.1, f32[1,2,16384]{2,1,0:T(2,128)} %refs_4_.1, f32[1,2,16384]{2,1,0:T(2,128)} %refs_5_.1, f32[1,2,16384]{2,1,0:T(2,128)} %refs_6_.1, ...), custom_call_target="tpu_custom_call" | custom-call | tf_op jit(solution)/shard_map/coupled/pallas_call | solution.py:639
  65.2 0.7 %unpack.1 = (f32[1,2,16384]{2,1,0:T(2,128)}, f32[1,2,512]{2,1,0:T(2,128)}) custom-call(f32[2,128,128]{2,1,0:T(8,128)S(1)} %get-tuple-element.4.planes_ref, f32[8,128]{1,0:T(8,128)S(1)} %get-tuple-element.5.rows_ref), custom_call_target="tpu_custom_call" | custom-call | tf_op jit(solution)/shard_map/unpack/pallas_call | solution.py:665

commit v4 on v3

--- a/solution.py
+++ b/solution.py
@@ -228,6 +228,41 @@
             return []
         return [send_planes((cx, vx, hx)[j], lo, hi, to, j + 4) for j in which]
 
+    sides = ((-1, 1, lax.rem(me, 2) == 0), (1, -1, lax.rem(me, 2) == 1))
+    assert reach == 2 and near == planes == 2 and n % 2 == 0
+
+    def when(mine, d, act):
+        @pl.when(jnp.logical_and(mine, there(d)))
+        def _():
+            act()
+
+    def rest_each(which, act):
+        for x, p, mine in sides:
+            for d in (x, p, 2 * p):
+                when(mine, d, lambda d=d: act(rest_copies(d, which)))
+
+    def handed_rest(x, p):
+        plane = depth - 1 if x < 0 else depth + planes
+        return [
+            rcopy(
+                buf.at[pl.ds(plane, 1)],
+                buf.at[pl.ds(plane - p * planes, 1)],
+                set_send.at[j + 4, at[x - p]],
+                set_recv.at[j + 4, at[x - p]],
+                {"sub": me + p},
+            )
+            for j, buf in enumerate((cx, vx, hx))
+        ]
+
+    def handed_halo(par, x, p):
+        return rcopy(
+            land.at[par, at[x]],
+            land.at[par, at[x - p]],
+            halo_send.at[par, at[x - p]],
+            halo_recv.at[par, at[x - p]],
+            {"sub": me + p},
+        )
+
     def surf_copies(to):
         return [
             rcopy(
@@ -451,11 +486,9 @@
         for i in range(half):
             exp_one[i : i + 1, :] = mixed[:, i * LANES : (i + 1) * LANES]
         exchange(False, par)
-        for d in offs:
-
-            @pl.when(there(d))
-            def _():
-                halo_copy(par, d, -d).start()
+        for x, p, mine in sides:
+            for d in (x, p, 2 * p):
+                when(mine, d, lambda d=d: halo_copy(par, d, -d).start())
 
         here = sample([temp])[0]
         for i in range(half):
@@ -467,10 +500,17 @@
         part_one[pl.ds(reach, n)] = part - jnp.where(mine, gain_t * own_temp[...], 0.0)
         for k in range(1, n):
             rs_copy(False, par, k, me).start()
+        for x, p, mine in sides:
+
+            def hand_on(x=x, p=p):
+                halo_copy(par, -x, x).wait_recv()
+                handed_halo(par, x, p).start()
+
+            when(mine, x, hand_on)
 
         @pl.when(first)
         def _():
-            each(offs, lambda d: starts(rest_copies(d, (2,))))
+            rest_each((2,), starts)
 
         rs_one[par, me] = part_one[pl.ds(me, span)]
 
@@ -480,12 +520,12 @@
             for d in offs:
                 hot_rows(d + reach)
 
-        for d in offs:
-
-            @pl.when(there(d))
-            def _():
-                halo_copy(par, d, -d).wait_send()
-                halo_copy(par, -d, d).wait_recv()
+        for x, p, mine in sides:
+            for d in (x, p, 2 * p):
+                when(mine, d, lambda d=d: halo_copy(par, d, -d).wait_send())
+            when(mine, x, lambda x=x, p=p: handed_halo(par, x, p).wait_send())
+            for d in (p, 2 * p, 2 * x):
+                when(mine, d, lambda d=d: halo_copy(par, -d, d).wait_recv())
 
         for k in range(1, n):
             rs_copy(False, par, k, lax.rem(me + n - k, n)).wait_recv()
@@ -502,7 +542,10 @@
         @pl.when(first)
         def _():
             each(offs, lambda d: arrivals(rest_copies(-d, (0, 1, 2))))
-            each(offs, lambda d: departures(rest_copies(d, (0, 1, 2)) + surf_copies(d)))
+            each(offs, lambda d: departures(surf_copies(d)))
+            rest_each((0, 1, 2), departures)
+            for x, p, mine in sides:
+                when(mine, x, lambda x=x, p=p: departures(handed_rest(x, p)))
 
         finish(False, par)
         return carry
@@ -538,7 +581,10 @@
     for k in range(near):
         step(pair[k % 2], pair[(k + 1) % 2], depth - near + k)
     each(beside, lambda d: mid_copy(d).start())
-    each(offs, lambda d: starts(surf_copies(d) + rest_copies(d, (0, 1))))
+    each(offs, lambda d: starts(surf_copies(d)))
+    rest_each((0, 1), starts)
+    for x, p, mine in sides:
+        when(mine, x, lambda x=x, p=p: starts(handed_rest(x, p)))
     each(beside, lambda d: mid_copy(-d).wait_recv())
     for d in beside:
         fa[pl.ds(depth + planes * d, planes)] = land[1, at[d]]

time: 66.1 us -> 65 us (0.983)
  Pallas kernels: 65.3 us -> 64.2 us
    pallas_call x1, Pallas kernels: 64.6 us -> 63.4 us  [local(): pl.pallas_call(body, name='coupled', out_shape=(pltpu.VMEM((planes, rows,...]
where the time goes in v4:
time: 65 us; the launch traced here: 64.8 us
  Pallas kernels  64.2 us (99%)
    pallas_call x1, Pallas kernels, local(): pl.pallas_call(body, name='coupled', out_shape=(pltpu.VMEM((planes, rows,...  63.4 us

profile of v4, /device:TPU:0, one launch (start us, length us, event | category | flops | bytes accessed | tf_op | source)
XLA Modules:
  0.0 64.8 jit_solution(13798078673687551496)
XLA Ops:
  0.6 63.4 %coupled.1 = (f32[2,128,128]{2,1,0:T(8,128)S(1)}, f32[8,128]{1,0:T(8,128)S(1)}) custom-call(s32[4]{0:T(128)} %refs_0_.1, s32[4]{0:T(128)} %refs_1_.1, s32[1,8]{1,0:T(1,128)} %refs_2_.1, f32[1,2,16384]{2,1,0:T(2,128)} %refs_3_.1, f32[1,2,16384]{2,1,0:T(2,128)} %refs_4_.1, f32[1,2,16384]{2,1,0:T(2,128)} %refs_5_.1, f32[1,2,16384]{2,1,0:T(2,128)} %refs_6_.1, ...), custom_call_target="tpu_custom_call" | custom-call | tf_op jit(solution)/shard_map/coupled/pallas_call | solution.py:685
  64.1 0.7 %unpack.1 = (f32[1,2,16384]{2,1,0:T(2,128)}, f32[1,2,512]{2,1,0:T(2,128)}) custom-call(f32[2,128,128]{2,1,0:T(8,128)S(1)} %get-tuple-element.4.planes_ref, f32[8,128]{1,0:T(8,128)S(1)} %get-tuple-element.5.rows_ref), custom_call_target="tpu_custom_call" | custom-call | tf_op jit(solution)/shard_map/unpack/pallas_call | solution.py:711

commit v5 on v4

--- a/solution.py
+++ b/solution.py
@@ -97,6 +97,7 @@
     targ_ref,
     maps,
     load_sem,
+    ready,
 ):
     planes = field_ref.shape[0]
     rows = fa.shape[1]
@@ -145,19 +146,32 @@
     for c in loads:
         c.start()
 
+    def signal(sem, dev):
+        pl.semaphore_signal(sem, inc=1, device_id=dev, device_id_type=pl.DeviceIdType.MESH)
+
+    def among(ds):
+        return sum(there(d).astype(jnp.int32) for d in ds)
+
+    def tell(sem, ds):
+        for d in ds:
+
+            @pl.when(there(d))
+            def _():
+                signal(sem, {"sub": me + d})
+
     barrier = pltpu.get_barrier_semaphore()
-    for k in range(1, n):
-        pl.semaphore_signal(
-            barrier, inc=1, device_id={"sub": lax.rem(me + k, n)}, device_id_type=pl.DeviceIdType.MESH
-        )
+    tell(barrier, offs)
     for k in range(1, groups):
-        for j in range(n):
-            pl.semaphore_signal(
-                barrier,
-                inc=1,
-                device_id={"grp": lax.rem(grp + k, groups), "sub": lax.rem(me + j, n)},
-                device_id_type=pl.DeviceIdType.MESH,
-            )
+        signal(barrier, {"grp": lax.rem(grp + k, groups)})
+    hops = [reach]
+    while 2 * hops[-1] < n:
+        hops.append(2 * hops[-1])
+
+    def hear(i):
+        pl.semaphore_wait(ready.at[i], among((-hops[i], hops[i])))
+
+    def pass_on(i):
+        tell(ready.at[i], (-hops[i], hops[i]))
 
     for border in (pl.ds(0, reach), pl.ds(reach + n, reach)):
         part_one[border] = jnp.zeros((reach, half, LANES), F32)
@@ -195,7 +209,7 @@
         return carry
 
     lax.fori_loop(0, rows // 8, unfold, 0)
-    pl.semaphore_wait(barrier, n * groups - 1)
+    pl.semaphore_wait(barrier, among(offs) + groups - 1)
 
     def send_planes(buf, lo, hi, to, j):
         slot = -to
@@ -304,6 +318,7 @@
 
     beside = (-1, 1)
     each(beside, lambda d: starts(first_copies(d)))
+    pass_on(0)
 
     partner = partner_ref[grp]
     count = count_ref[0, me]
@@ -576,7 +591,16 @@
         finish(True, par)
 
     pair = (fa, fb)
+    hear(0)
+    for i in range(1, len(hops)):
+        pass_on(i)
+        if i < len(hops) - 1:
+            hear(i)
     each(beside, lambda d: arrivals(first_copies(-d)))
+    if len(hops) > 1:
+        hear(len(hops) - 1)
+    for k in range(1, groups):
+        signal(ready.at[len(hops)], {"grp": lax.rem(grp + k, groups)})
     each(beside, lambda d: departures(first_copies(d)))
     for k in range(near):
         step(pair[k % 2], pair[(k + 1) % 2], depth - near + k)
@@ -592,6 +616,7 @@
     for k in range(near):
         step(pair[k % 2], pair[(k + 1) % 2], depth - near + k)
 
+    pl.semaphore_wait(ready.at[len(hops)], groups - 1)
     lax.fori_loop(0, COUPLE - 1, couple, 0)
     final()
 
@@ -677,6 +702,7 @@
             pltpu.VMEM((cap, LANES), jnp.int32),
             pltpu.VMEM((cap, LANES, LANES), F32),
             dma((11,)),
+            pltpu.SemaphoreType.REGULAR((n.bit_length() + 1,)),
         ]
 
         def body(*refs):

time: 65 us -> 63.9 us (0.983)
  Pallas kernels: 64.2 us -> 63.1 us
    pallas_call x1, Pallas kernels: 63.4 us -> 62.3 us  [local(): pl.pallas_call(body, name='coupled', out_shape=(pltpu.VMEM((planes, rows,...]
where the time goes in v5:
time: 63.9 us; the launch traced here: 63.7 us
  Pallas kernels  63.1 us (99%)
  between operations  0.64 us (1%)
    pallas_call x1, Pallas kernels, local(): pl.pallas_call(body, name='coupled', out_shape=(pltpu.VMEM((planes, rows,...  62.3 us

profile of v5, /device:TPU:0, one launch (start us, length us, event | category | flops | bytes accessed | tf_op | source)
XLA Modules:
  0.0 63.7 jit_solution(3638323380330106594)
XLA Ops:
  0.6 62.3 %coupled.1 = (f32[2,128,128]{2,1,0:T(8,128)S(1)}, f32[8,128]{1,0:T(8,128)S(1)}) custom-call(s32[4]{0:T(128)} %refs_0_.1, s32[4]{0:T(128)} %refs_1_.1, s32[1,8]{1,0:T(1,128)} %refs_2_.1, f32[1,2,16384]{2,1,0:T(2,128)} %refs_3_.1, f32[1,2,16384]{2,1,0:T(2,128)} %refs_4_.1, f32[1,2,16384]{2,1,0:T(2,128)} %refs_5_.1, f32[1,2,16384]{2,1,0:T(2,128)} %refs_6_.1, ...), custom_call_target="tpu_custom_call" | custom-call | tf_op jit(solution)/shard_map/coupled/pallas_call | solution.py:711
  63.0 0.7 %unpack.1 = (f32[1,2,16384]{2,1,0:T(2,128)}, f32[1,2,512]{2,1,0:T(2,128)}) custom-call(f32[2,128,128]{2,1,0:T(8,128)S(1)} %get-tuple-element.4.planes_ref, f32[8,128]{1,0:T(8,128)S(1)} %get-tuple-element.5.rows_ref), custom_call_target="tpu_custom_call" | custom-call | tf_op jit(solution)/shard_map/unpack/pallas_call | solution.py:737

commit v6 on v5

--- a/solution.py
+++ b/solution.py
@@ -408,13 +408,15 @@
             {"grp": lax.rem(grp + k, groups), "sub": peer},
         )
 
-    def rs_copy(two, par, k, sender):
-        peer = lax.rem(me + k, n)
+    def peers():
+        return [lax.rem(me + jnp.where(upper, k, n - k), n) for k in range(1, n)]
+
+    def rs_copy(two, par, peer, sender):
         if two:
             src, dst = part_two.at[peer], rs_two.at[sender]
         else:
             src, dst = part_one.at[pl.ds(peer, span)], rs_one.at[par, sender]
-        return rcopy(src, dst, rs_send.at[par, k - 1], rs_recv.at[par, k - 1], {"sub": peer})
+        return rcopy(src, dst, rs_send.at[par, peer], rs_recv.at[par, sender], {"sub": peer})
 
     def sample(values):
         lhs = []
@@ -485,8 +487,8 @@
         for j in range(n):
             for k in range(1, groups):
                 ex_copy(two, par, k, j, me).wait_send()
-        for k in range(1, n):
-            rs_copy(two, par, k, me).wait_send()
+        for peer in peers():
+            rs_copy(two, par, peer, me).wait_send()
 
     def couple(it, carry):
         par = lax.rem(it, 2)
@@ -513,8 +515,8 @@
         part = patches([srcs.reshape(blocks, LANES)])[0].reshape(n, half, LANES)
         mine = iota((n, half, LANES), 0) == me
         part_one[pl.ds(reach, n)] = part - jnp.where(mine, gain_t * own_temp[...], 0.0)
-        for k in range(1, n):
-            rs_copy(False, par, k, me).start()
+        for peer in peers():
+            rs_copy(False, par, peer, me).start()
         for x, p, mine in sides:
 
             def hand_on(x=x, p=p):
@@ -542,8 +544,8 @@
             for d in (p, 2 * p, 2 * x):
                 when(mine, d, lambda d=d: halo_copy(par, -d, d).wait_recv())
 
-        for k in range(1, n):
-            rs_copy(False, par, k, lax.rem(me + n - k, n)).wait_recv()
+        for peer in peers():
+            rs_copy(False, par, me, peer).wait_recv()
         inc = rs_one[par, 0]
         for j in range(1, n):
             inc = inc + rs_one[par, j]
@@ -576,11 +578,11 @@
         src = chosen(True, par)
         parts = patches([src[:, q * half : (q + 1) * half].reshape(blocks, LANES) for q in range(2)])
         part_two[...] = jnp.concatenate([x.reshape(n, half, LANES) for x in parts], axis=1)
-        for k in range(1, n):
-            rs_copy(True, par, k, me).start()
+        for peer in peers():
+            rs_copy(True, par, peer, me).start()
         rs_two[me] = part_two[me]
-        for k in range(1, n):
-            rs_copy(True, par, k, lax.rem(me + n - k, n)).wait_recv()
+        for peer in peers():
+            rs_copy(True, par, me, peer).wait_recv()
         iface = rs_two[0]
         for j in range(1, n):
             iface = iface + rs_two[j]
@@ -687,8 +689,8 @@
             dma((9, nd)),
             dma((2, groups - 1, n)),
             dma((2, groups - 1, n)),
-            dma((2, n - 1)),
-            dma((2, n - 1)),
+            dma((2, n)),
+            dma((2, n)),
             dma((2, nd)),
             dma((2, nd)),
             pltpu.SMEM(group_kind.shape, jnp.int32),

time: 63.9 us -> 63.1 us (0.987)
  Pallas kernels: 63.1 us -> 62.3 us
    pallas_call x1, Pallas kernels: 62.3 us -> 61.6 us  [local(): pl.pallas_call(body, name='coupled', out_shape=(pltpu.VMEM((planes, rows,...]
where the time goes in v6:
time: 63.1 us; the launch traced here: 62.9 us
  Pallas kernels  62.3 us (99%)
  between operations  0.64 us (1%)
    pallas_call x1, Pallas kernels, local(): pl.pallas_call(body, name='coupled', out_shape=(pltpu.VMEM((planes, rows,...  61.6 us

profile of v6, /device:TPU:0, one launch (start us, length us, event | category | flops | bytes accessed | tf_op | source)
XLA Modules:
  0.0 62.9 jit_solution(5680498758891952549)
XLA Ops:
  0.6 61.6 %coupled.1 = (f32[2,128,128]{2,1,0:T(8,128)S(1)}, f32[8,128]{1,0:T(8,128)S(1)}) custom-call(s32[4]{0:T(128)} %refs_0_.1, s32[4]{0:T(128)} %refs_1_.1, s32[1,8]{1,0:T(1,128)} %refs_2_.1, f32[1,2,16384]{2,1,0:T(2,128)} %refs_3_.1, f32[1,2,16384]{2,1,0:T(2,128)} %refs_4_.1, f32[1,2,16384]{2,1,0:T(2,128)} %refs_5_.1, f32[1,2,16384]{2,1,0:T(2,128)} %refs_6_.1, ...), custom_call_target="tpu_custom_call" | custom-call | tf_op jit(solution)/shard_map/coupled/pallas_call | solution.py:713
  62.2 0.7 %unpack.1 = (f32[1,2,16384]{2,1,0:T(2,128)}, f32[1,2,512]{2,1,0:T(2,128)}) custom-call(f32[2,128,128]{2,1,0:T(8,128)S(1)} %get-tuple-element.4.planes_ref, f32[8,128]{1,0:T(8,128)S(1)} %get-tuple-element.5.rows_ref), custom_call_target="tpu_custom_call" | custom-call | tf_op jit(solution)/shard_map/unpack/pallas_call | solution.py:739

commit v7 on v6

--- a/solution.py
+++ b/solution.py
@@ -507,6 +507,11 @@
             for d in (x, p, 2 * p):
                 when(mine, d, lambda d=d: halo_copy(par, d, -d).start())
 
+        @pl.when(first)
+        def _():
+            rest_each((1,), starts)
+
+
         here = sample([temp])[0]
         for i in range(half):
             own_temp[i : i + 1, :] = here[:, i * LANES : (i + 1) * LANES]
@@ -608,7 +613,7 @@
         step(pair[k % 2], pair[(k + 1) % 2], depth - near + k)
     each(beside, lambda d: mid_copy(d).start())
     each(offs, lambda d: starts(surf_copies(d)))
-    rest_each((0, 1), starts)
+    rest_each((0,), starts)
     for x, p, mine in sides:
         when(mine, x, lambda x=x, p=p: starts(handed_rest(x, p)))
     each(beside, lambda d: mid_copy(-d).wait_recv())

time: 63.1 us -> 62.4 us (0.989)
  Pallas kernels: 62.3 us -> 61.6 us
    pallas_call x1, Pallas kernels: 61.6 us -> 60.9 us  [local(): pl.pallas_call(body, name='coupled', out_shape=(pltpu.VMEM((planes, rows,...]
where the time goes in v7:
time: 62.4 us; the launch traced here: 62.3 us
  Pallas kernels  61.6 us (99%)
  between operations  0.64 us (1%)
    pallas_call x1, Pallas kernels, local(): pl.pallas_call(body, name='coupled', out_shape=(pltpu.VMEM((planes, rows,...  60.9 us

profile of v7, /device:TPU:0, one launch (start us, length us, event | category | flops | bytes accessed | tf_op | source)
XLA Modules:
  0.0 62.3 jit_solution(13400676895689301330)
XLA Ops:
  0.6 60.9 %coupled.1 = (f32[2,128,128]{2,1,0:T(8,128)S(1)}, f32[8,128]{1,0:T(8,128)S(1)}) custom-call(s32[4]{0:T(128)} %refs_0_.1, s32[4]{0:T(128)} %refs_1_.1, s32[1,8]{1,0:T(1,128)} %refs_2_.1, f32[1,2,16384]{2,1,0:T(2,128)} %refs_3_.1, f32[1,2,16384]{2,1,0:T(2,128)} %refs_4_.1, f32[1,2,16384]{2,1,0:T(2,128)} %refs_5_.1, f32[1,2,16384]{2,1,0:T(2,128)} %refs_6_.1, ...), custom_call_target="tpu_custom_call" | custom-call | tf_op jit(solution)/shard_map/coupled/pallas_call | solution.py:718
  61.5 0.7 %unpack.1 = (f32[1,2,16384]{2,1,0:T(2,128)}, f32[1,2,512]{2,1,0:T(2,128)}) custom-call(f32[2,128,128]{2,1,0:T(8,128)S(1)} %get-tuple-element.4.planes_ref, f32[8,128]{1,0:T(8,128)S(1)} %get-tuple-element.5.rows_ref), custom_call_target="tpu_custom_call" | custom-call | tf_op jit(solution)/shard_map/unpack/pallas_call | solution.py:744

commit v8 on v7

--- a/solution.py
+++ b/solution.py
@@ -98,6 +98,8 @@
     maps,
     load_sem,
     ready,
+    ax,
+    bx,
 ):
     planes = field_ref.shape[0]
     rows = fa.shape[1]
@@ -370,12 +372,16 @@
 
     block_of_slot = iota((blocks, cap * LANES), 0)
 
+    def gather_terms(zs):
+        for z in zs:
+            ax[z] = 1.0 - 6.0 * cx[z] - vx[z]
+            bx[z] = cx[z] + vx[z]
+
     def step(src, dst, k):
         for z in range(k + 1, ext - k - 1):
             c = src[z]
-            dn = src[z - 1]
-            lap = src[z + 1] + dn + in_plane(c) - 6.0 * c
-            dst[z] = c + cx[z] * lap - vx[z] * (c - dn) + hx[z] * (1.0 + jnp.tanh(c))
+            rest = hx[z] * (1.0 + jnp.tanh(c))
+            dst[z] = ax[z] * c + cx[z] * (src[z + 1] + in_plane(c)) + (bx[z] * src[z - 1] + rest)
 
     def spread(slot, inc):
         lhs = []
@@ -564,6 +570,7 @@
         @pl.when(first)
         def _():
             each(offs, lambda d: arrivals(rest_copies(-d, (0, 1, 2))))
+            gather_terms([z for z in range(1, ext - 1) if z not in close])
             each(offs, lambda d: departures(surf_copies(d)))
             rest_each((0, 1, 2), departures)
             for x, p, mine in sides:
@@ -609,6 +616,8 @@
     for k in range(1, groups):
         signal(ready.at[len(hops)], {"grp": lax.rem(grp + k, groups)})
     each(beside, lambda d: departures(first_copies(d)))
+    close = range(depth - near + 1, depth + planes + near - 1)
+    gather_terms(close)
     for k in range(near):
         step(pair[k % 2], pair[(k + 1) % 2], depth - near + k)
     each(beside, lambda d: mid_copy(d).start())
@@ -710,6 +719,8 @@
             pltpu.VMEM((cap, LANES, LANES), F32),
             dma((11,)),
             pltpu.SemaphoreType.REGULAR((n.bit_length() + 1,)),
+            pltpu.VMEM((ext, rows, LANES), F32),
+            pltpu.VMEM((ext, rows, LANES), F32),
         ]
 
         def body(*refs):

time: 62.4 us -> 62.1 us (level)
  no operation moved by 1% of the time
where the time goes in v8:
time: 62.1 us; the launch traced here: 61.9 us
  Pallas kernels  61.3 us (99%)
  between operations  0.64 us (1%)
    pallas_call x1, Pallas kernels, local(): pl.pallas_call(body, name='coupled', out_shape=(pltpu.VMEM((planes, rows,...  60.5 us

profile of v8, /device:TPU:0, one launch (start us, length us, event | category | flops | bytes accessed | tf_op | source)
XLA Modules:
  0.0 61.9 jit_solution(10297532702402405701)
XLA Ops:
  0.6 60.5 %coupled.1 = (f32[2,128,128]{2,1,0:T(8,128)S(1)}, f32[8,128]{1,0:T(8,128)S(1)}) custom-call(s32[4]{0:T(128)} %refs_0_.1, s32[4]{0:T(128)} %refs_1_.1, s32[1,8]{1,0:T(1,128)} %refs_2_.1, f32[1,2,16384]{2,1,0:T(2,128)} %refs_3_.1, f32[1,2,16384]{2,1,0:T(2,128)} %refs_4_.1, f32[1,2,16384]{2,1,0:T(2,128)} %refs_5_.1, f32[1,2,16384]{2,1,0:T(2,128)} %refs_6_.1, ...), custom_call_target="tpu_custom_call" | custom-call | tf_op jit(solution)/shard_map/coupled/pallas_call | solution.py:729
  61.2 0.7 %unpack.1 = (f32[1,2,16384]{2,1,0:T(2,128)}, f32[1,2,512]{2,1,0:T(2,128)}) custom-call(f32[2,128,128]{2,1,0:T(8,128)S(1)} %get-tuple-element.4.planes_ref, f32[8,128]{1,0:T(8,128)S(1)} %get-tuple-element.5.rows_ref), custom_call_target="tpu_custom_call" | custom-call | tf_op jit(solution)/shard_map/unpack/pallas_call | solution.py:755

commit v9 on v8

--- a/solution.py
+++ b/solution.py
@@ -547,6 +547,8 @@
             each(offs, lambda d: arrivals(surf_copies(-d)))
             for d in offs:
                 hot_rows(d + reach)
+            each(offs, lambda d: arrivals(rest_copies(-d, (0, 1))))
+            gather_terms([z for z in range(1, ext - 1) if z not in close])
 
         for x, p, mine in sides:
             for d in (x, p, 2 * p):
@@ -569,8 +571,7 @@
 
         @pl.when(first)
         def _():
-            each(offs, lambda d: arrivals(rest_copies(-d, (0, 1, 2))))
-            gather_terms([z for z in range(1, ext - 1) if z not in close])
+            each(offs, lambda d: arrivals(rest_copies(-d, (2,))))
             each(offs, lambda d: departures(surf_copies(d)))
             rest_each((0, 1, 2), departures)
             for x, p, mine in sides:

time: 62.1 us -> 62.1 us (level)
  no operation moved by 1% of the time
where the time goes in v9:
time: 62.1 us; the launch traced here: 62 us
  Pallas kernels  61.3 us (99%)
  between operations  0.64 us (1%)
    pallas_call x1, Pallas kernels, local(): pl.pallas_call(body, name='coupled', out_shape=(pltpu.VMEM((planes, rows,...  60.6 us

profile of v9, /device:TPU:0, one launch (start us, length us, event | category | flops | bytes accessed | tf_op | source)
XLA Modules:
  0.0 62.0 jit_solution(7972514975990504601)
XLA Ops:
  0.6 60.6 %coupled.1 = (f32[2,128,128]{2,1,0:T(8,128)S(1)}, f32[8,128]{1,0:T(8,128)S(1)}) custom-call(s32[4]{0:T(128)} %refs_0_.1, s32[4]{0:T(128)} %refs_1_.1, s32[1,8]{1,0:T(1,128)} %refs_2_.1, f32[1,2,16384]{2,1,0:T(2,128)} %refs_3_.1, f32[1,2,16384]{2,1,0:T(2,128)} %refs_4_.1, f32[1,2,16384]{2,1,0:T(2,128)} %refs_5_.1, f32[1,2,16384]{2,1,0:T(2,128)} %refs_6_.1, ...), custom_call_target="tpu_custom_call" | custom-call | tf_op jit(solution)/shard_map/coupled/pallas_call | solution.py:730
  61.2 0.7 %unpack.1 = (f32[1,2,16384]{2,1,0:T(2,128)}, f32[1,2,512]{2,1,0:T(2,128)}) custom-call(f32[2,128,128]{2,1,0:T(8,128)S(1)} %get-tuple-element.4.planes_ref, f32[8,128]{1,0:T(8,128)S(1)} %get-tuple-element.5.rows_ref), custom_call_target="tpu_custom_call" | custom-call | tf_op jit(solution)/shard_map/unpack/pallas_call | solution.py:756
